TPU v7x, 32 devices: a whole 2x2x4 slice. The times are simulated.
32 devices in a mesh: shard: 8 (over z, x), model: 4 (over y, core).
Axes of the slice: x: 2, y: 2, z: 4, core: 2. Of those that a mesh axis runs over, the one named last changes fastest.
Arguments:
- grad_stack: float32 [64, 128, 2048], P(None, 'shard', 'model'), may hold values from -6 to 6
- moment_stack: float32 [64, 128, 2048], P(None, 'shard', 'model'), may hold values from -6 to 6
- weight_stack: float32 [64, 128, 2048], P(None, 'shard', 'model'), may hold values from -0.1875 to 0.1875
Outputs:
- new_weights: float32 [64, 128, 2048], P(None, 'shard', 'model')
- new_momentum: float32 [64, 128, 2048], P(None, 'shard', 'model')
All inputs are finite; a program needn't handle non-finite values.
Results may differ from a plain program's by a relative error of at most 0.00021.
Values sent between devices are 32-bit elements; how exact they have to be, the bound alone decides.
No kernel may reach another device: no remote copies, remote signals or barrier semaphores. Data moves between devices by JAX's collectives and lax.ppermute only.
A program may use at most 64 MiB of HBM per device.

v0:
```python
import jax
import jax.numpy as jnp
from jax import lax
from jax.sharding import PartitionSpec as P

ITERS = 5


hold_rate = 0.95
learn_rate = 1.0
decay_rate = 0.1


def on_device(grad_stack, moment_stack, weight_stack):
    new_momentum = hold_rate * moment_stack + grad_stack
    moved = lax.all_to_all(new_momentum, "shard", split_axis=0, concat_axis=1, tiled=True)
    whole = lax.all_to_all(moved, "model", split_axis=0, concat_axis=2, tiled=True)
    iterate = whole * lax.rsqrt(jnp.sum(whole * whole, axis=(1, 2), keepdims=True) + 1e-06)
    for step in range(ITERS):
        gram = jnp.einsum("mik,mjk->mij", iterate, iterate, precision=lax.Precision.HIGHEST)
        mixed = -4.775 * gram + 2.0315 * jnp.einsum(
            "mij,mjk->mik", gram, gram, precision=lax.Precision.HIGHEST
        )
        iterate = 3.4445 * iterate + jnp.einsum(
            "mij,mjk->mik", mixed, iterate, precision=lax.Precision.HIGHEST
        )
    iterate = lax.all_to_all(iterate, "model", split_axis=2, concat_axis=0, tiled=True)
    back = lax.all_to_all(iterate, "shard", split_axis=1, concat_axis=0, tiled=True)
    new_weights = (1.0 - learn_rate * decay_rate) * weight_stack - learn_rate * back
    return (new_weights, new_momentum)


def solution(mesh):
    in_specs = (P(None, "shard", "model"), P(None, "shard", "model"), P(None, "shard", "model"))
    out_specs = (P(None, "shard", "model"), P(None, "shard", "model"))
    return jax.shard_map(
        on_device, mesh=mesh, in_specs=in_specs, out_specs=out_specs, check_vma=False
    )
```

profile of v0, /device:TPU:0, one launch (start us, length us, event | category | flops | bytes accessed | tf_op | source)
XLA Modules:
  0.0 201.4 jit_solution(9015392029939846904)
XLA Ops:
  0.6 2.7 %multiply_add_fusion = f32[64,16,512]{2,1,0:T(8,128)S(1)} fusion(f32[64,16,512]{2,1,0:T(8,128)} %param.3, f32[64,16,512]{2,1,0:T(8,128)} %param.4), kind=kLoop, calls=%fused_computation.7 | loop fusion | flops 1048576 | bytes 6291456 | tf_op jit(solution)/shard_map/add | solution.py:15
  3.3 0.0 copy-start
  3.4 55.3 %all_to_all.72 = f32[64,16,512]{2,1,0:T(8,128)S(1)} all-to-all(f32[64,16,512]{2,1,0:T(8,128)S(1)} %multiply_add_fusion), channel_id=1, replica_groups=mesh['shard'=8,'model'=4] {'shard'}, dimensions={0} | all-to-all | bytes 4194304 | tf_op jit(solution)/shard_map/all_to_all | solution.py:16
  58.7 0.0 copy-done
  58.7 0.2 copy.17
  58.9 28.3 %all_to_all.73 = f32[8,128,512]{2,1,0:T(8,128)S(1)} all-to-all(f32[8,128,512]{2,1,0:T(8,128)S(1)} %bitcast.49), channel_id=1, replica_groups=mesh['shard'=8,'model'=4] {'model'}, dimensions={0} | all-to-all | bytes 4194304 | tf_op jit(solution)/shard_map/all_to_all | solution.py:17
  87.1 0.4 multiply_reduce_fusion
  87.5 0.2 copy.26
  87.7 2.3 %fusion = f32[2,128,128]{2,1,0:T(8,128)S(1)} fusion(f32[2,128,2048]{2,1,0:T(8,128)S(1)} %bitcast.45, f32[2]{0:T(128)S(1)} %add_rsqrt_fusion), kind=kOutput, calls=%fused_computation.8 | convolution fusion | flops 805830656 | bytes 2228232 | tf_op jit(solution)/shard_map/mik,mjk->mij/dot_general | solution.py:20
  90.0 0.3 fusion.7
  90.3 2.1 %convolution_add_fusion.4 = f32[2,128,2048]{2,1,0:T(8,128)S(1)} fusion(f32[2,128,128]{2,1,0:T(8,128)S(1)} %fusion.7, f32[2,128,2048]{2,1,0:T(8,128)S(1)} %bitcast.46, f32[2]{0:T(128)S(1)} %add_rsqrt_fusion), kind=kOutput, calls=%fused_computation.4 | convolution fusion | flops 807403520 | bytes 4325384 | tf_op jit(solution)/shard_map/mij,mjk->mik/dot_general | solution.py:24
  92.4 2.0 %fusion.10 = f32[2,128,128]{2,1,0:T(8,128)S(1)} fusion(f32[2,128,2048]{2,1,0:T(8,128)S(1)} %convolution_add_fusion.4), kind=kOutput, calls=%fused_computation.24 | convolution fusion | flops 805306368 | bytes 2228224 | tf_op jit(solution)/shard_map/mik,mjk->mij/dot_general | solution.py:20
  94.5 0.3 fusion.6
  94.7 2.1 %convolution_add_fusion.3 = f32[2,128,2048]{2,1,0:T(8,128)S(1)} fusion(f32[2,128,128]{2,1,0:T(8,128)S(1)} %fusion.6, f32[2,128,2048]{2,1,0:T(8,128)S(1)} %convolution_add_fusion.4), kind=kOutput, calls=%fused_computation.3 | convolution fusion | flops 806354944 | bytes 4325376 | tf_op jit(solution)/shard_map/mij,mjk->mik/dot_general | solution.py:24
  96.8 2.0 %fusion.11 = f32[2,128,128]{2,1,0:T(8,128)S(1)} fusion(f32[2,128,2048]{2,1,0:T(8,128)S(1)} %convolution_add_fusion.3), kind=kOutput, calls=%fused_computation.25 | convolution fusion | flops 805306368 | bytes 2228224 | tf_op jit(solution)/shard_map/mik,mjk->mij/dot_general | solution.py:20
  98.9 0.3 fusion.5
  99.2 2.3 %convolution_add_fusion.2 = f32[2,128,2048]{2,1,0:T(8,128)S(1)} fusion(f32[2,128,128]{2,1,0:T(8,128)S(1)} %fusion.5, f32[2,128,2048]{2,1,0:T(8,128)S(1)} %convolution_add_fusion.3), kind=kOutput, calls=%fused_computation.2 | convolution fusion | flops 806354944 | bytes 4325376 | tf_op jit(solution)/shard_map/mij,mjk->mik/dot_general | solution.py:24
  101.5 2.0 %fusion.12 = f32[2,128,128]{2,1,0:T(8,128)S(1)} fusion(f32[2,128,2048]{2,1,0:T(8,128)S(1)} %convolution_add_fusion.2), kind=kOutput, calls=%fused_computation.26 | convolution fusion | flops 805306368 | bytes 2228224 | tf_op jit(solution)/shard_map/mik,mjk->mij/dot_general | solution.py:20
  103.5 0.3 fusion.4
  103.8 2.1 %convolution_add_fusion.1 = f32[2,128,2048]{2,1,0:T(8,128)S(1)} fusion(f32[2,128,128]{2,1,0:T(8,128)S(1)} %fusion.4, f32[2,128,2048]{2,1,0:T(8,128)S(1)} %convolution_add_fusion.2), kind=kOutput, calls=%fused_computation.1 | convolution fusion | flops 806354944 | bytes 4325376 | tf_op jit(solution)/shard_map/mij,mjk->mik/dot_general | solution.py:24
  105.9 2.0 %fusion.13 = f32[2,128,128]{2,1,0:T(8,128)S(1)} fusion(f32[2,128,2048]{2,1,0:T(8,128)S(1)} %convolution_add_fusion.1), kind=kOutput, calls=%fused_computation.27 | convolution fusion | flops 805306368 | bytes 2228224 | tf_op jit(solution)/shard_map/mik,mjk->mij/dot_general | solution.py:20
  107.9 0.3 fusion.3
  108.2 2.1 %convolution_add_fusion = f32[2,128,2048]{2,1,0:T(8,128)S(1)} fusion(f32[2,128,128]{2,1,0:T(8,128)S(1)} %fusion.3, f32[2,128,2048]{2,1,0:T(8,128)S(1)} %convolution_add_fusion.1), kind=kOutput, calls=%fused_computation | convolution fusion | flops 806354944 | bytes 4325376 | tf_op jit(solution)/shard_map/mij,mjk->mik/dot_general | solution.py:24
  110.3 2.3 %copy.19 = f32[2,128,2048]{1,0,2:T(2,128)} copy(f32[2,128,2048]{2,1,0:T(8,128)S(1)} %convolution_add_fusion) | data formatting | bytes 4194304 | tf_op jit(solution)/shard_map/add | solution.py:24
  112.6 29.2 %all_to_all.74 = f32[2,128,2048]{1,0,2:T(2,128)S(1)} all-to-all(f32[2,128,2048]{1,0,2:T(2,128)} %copy.19), channel_id=1, replica_groups=mesh['shard'=8,'model'=4] {'model'}, dimensions={2} | all-to-all | bytes 4194304 | tf_op jit(solution)/shard_map/all_to_all | solution.py:27
  141.8 0.1 copy.20
  142.0 1.8 copy.21
  143.8 2.8 %copy.22 = f32[8,128,512]{2,0,1:T(8,128)S(1)} copy(f32[8,128,512]{2,1,0:T(8,128)} %bitcast.51) | data formatting | bytes 4194304 | tf_op jit(solution)/shard_map/all_to_all | solution.py:27
  146.6 51.4 %all_to_all.75 = f32[8,128,512]{2,0,1:T(8,128)S(1)} all-to-all(f32[8,128,512]{2,0,1:T(8,128)S(1)} %copy.22), channel_id=1, replica_groups=mesh['shard'=8,'model'=4] {'shard'}, dimensions={1} | all-to-all | bytes 4194304 | tf_op jit(solution)/shard_map/all_to_all | solution.py:28
  198.0 0.0 copy-start.1
  198.0 1.2 copy.24
  199.2 0.4 copy-done.1
  199.5 1.8 bitcast_subtract_fusion
  (1 shorter events, 0.0 us)
Async XLA Ops:
  3.3 55.3 %copy-start = (f32[64,16,512]{2,1,0:T(8,128)}, f32[64,16,512]{2,1,0:T(8,128)S(1)}, u32[]{:S(2)}) copy-start(f32[64,16,512]{2,1,0:T(8,128)S(1)} %multiply_add_fusion) | copy-start | bytes 6291460
  198.0 1.6 copy-start.1
where the time goes:
time: 202 us; the launch traced here: 201 us
  blocking collectives  164 us (81%)
  matrix products  22.4 us (11%)
  local copies, waits for them, and re-layouts  9.08 us (4%)
  other arithmetic  4.91 us (2%)
    all_to_all x1, blocking collectives, on_device(): lax.all_to_all(new_momentum, 'shard', split_axis=0, concat_axis=1, tiled=...  55.3 us
    all_to_all x1, blocking collectives, on_device(): lax.all_to_all(iterate, 'shard', split_axis=1, concat_axis=0, tiled=True)  51.4 us
    all_to_all x1, blocking collectives, on_device(): lax.all_to_all(iterate, 'model', split_axis=2, concat_axis=0, tiled=True)  29.2 us
    all_to_all x1, blocking collectives, on_device(): lax.all_to_all(moved, 'model', split_axis=0, concat_axis=2, tiled=True)  28.3 us
    dot_general x5, matrix products, on_device(): jnp.einsum('mij,mjk->mik', mixed, iterate, precision=lax.Precision.HIGHEST)  10.7 us
    dot_general x5, matrix products, on_device(): jnp.einsum('mik,mjk->mij', iterate, iterate, precision=lax.Precision.HIGH...  10.4 us
    all_to_all x3, local copies, waits for them, and re-layouts, on_device(): lax.all_to_all(iterate, 'model', split_axis=2, concat_axis=0, tiled=True)  4.76 us

commit v1 on v0

v1 whole, which is shorter than its diff:
```python
import jax
import jax.numpy as jnp
from jax import lax
from jax.sharding import PartitionSpec as P

hold_rate = 0.95
learn_rate = 1.0
decay_rate = 0.1
HI = lax.Precision.HIGHEST
A0, A1, A2 = 3.4445, -4.775, 2.0315


def mm(a, b):
    return jnp.einsum("mij,mjk->mik", a, b, precision=HI)


def gram_of(x):
    return jnp.einsum("mik,mjk->mij", x, x, precision=HI)


def factor(g, eye):
    return A0 * eye + A1 * g + A2 * mm(g, g)


def chain(g, steps, eye):
    total = None
    for step in range(steps):
        p = factor(g, eye)
        total = p if total is None else mm(p, total)
        if step < steps - 1:
            g = mm(mm(p, g), p)
    return total


def summed_over_model(g, model):
    half = g.shape[0] // 2
    bit = lax.axis_index("model") % 2
    keep = lax.dynamic_slice_in_dim(g, bit * half, half, 0)
    send = lax.dynamic_slice_in_dim(g, (1 - bit) * half, half, 0)
    own = keep + lax.ppermute(send, "model", [(i, i ^ 1) for i in range(model)])
    dist = 2
    while dist < model:
        own = own + lax.ppermute(own, "model", [(i, i ^ dist) for i in range(model)])
        dist *= 2
    return own


def joined(own, model):
    bit = lax.axis_index("model") % 2
    other = lax.ppermute(own, "model", [(i, i ^ 1) for i in range(model)])
    return jnp.where(bit == 0, jnp.concatenate([own, other]), jnp.concatenate([other, own]))


def process(x, model, first=2, last=3):
    eye = jnp.eye(x.shape[1], dtype=jnp.float32)
    g = summed_over_model(gram_of(x), model)
    r = lax.rsqrt(jnp.einsum("mii->m", g) + 1e-06)[:, None, None]
    q = chain(g * (r * r), first, eye) * r
    x = mm(joined(q, model), x)
    if last:
        g = summed_over_model(gram_of(x), model)
        x = mm(joined(chain(g, last, eye), model), x)
    return x


def make(mesh, K=1, first=2, last=3):
    shards, model = mesh.shape["shard"], mesh.shape["model"]

    def on_device(grad_stack, moment_stack, weight_stack):
        new_momentum = hold_rate * moment_stack + grad_stack
        mats, rows, cols = new_momentum.shape
        x = lax.all_to_all(new_momentum, "shard", split_axis=0, concat_axis=1, tiled=True)
        x = process(x, model, first, last)
        back = lax.all_to_all(x, "shard", split_axis=1, concat_axis=0, tiled=True)
        new_weights = (1.0 - learn_rate * decay_rate) * weight_stack - learn_rate * back
        return (new_weights, new_momentum)
    return on_device


def solution(mesh):
    spec = P(None, "shard", "model")
    return jax.shard_map(
        make(mesh), mesh=mesh, in_specs=(spec,) * 3, out_specs=(spec,) * 2, check_vma=False
    )
```

time: 202 us -> 158 us (0.78)
  blocking collectives: 164 us -> 51.9 us
  waiting for transfers between devices: 0 us -> 67.8 us
  starting transfers between devices: 0 us -> 10.8 us
  matrix products: 22.4 us -> 13.6 us
  local copies, waits for them, and re-layouts: 9.08 us -> 5.95 us
    all_to_all x4 -> x1, blocking collectives: 164 us -> 51.9 us  [on_device(): back = lax.all_to_all(x, 'shard', split_axis=1, concat_axis=0, tiled=True)]
    all_to_all x0 -> x1, waiting for transfers between devices: none -> 48.2 us  [on_device(): lax.all_to_all(new_momentum, 'shard', split_axis=0, concat_axis=1, tiled=...]
    ppermute x0 -> x6, waiting for transfers between devices: none -> 19.6 us  [the longest x2 13.6 us: summed_over_model(): lax.ppermute(own, 'model', [(i, i ^ dist) for i in range(model)])]
    dot_general x15 -> x18, matrix products: 22.4 us -> 13.6 us  [the longest x16 9.47 us: mm(): return jnp.einsum('mij,mjk->mik', a, b, precision=HI)]
    all_to_all x0 -> x1, starting transfers between devices: none -> 7.28 us  [on_device(): lax.all_to_all(new_momentum, 'shard', split_axis=0, concat_axis=1, tiled=...]
    all_to_all x5 -> x1, local copies, waits for them, and re-layouts: 6.19 us -> 1.2 us  [on_device(): back = lax.all_to_all(x, 'shard', split_axis=1, concat_axis=0, tiled=True)]
    ppermute x0 -> x6, starting transfers between devices: none -> 3.57 us  [the longest x2 3.16 us: summed_over_model(): lax.ppermute(own, 'model', [(i, i ^ dist) for i in range(model)])]
    add x1 -> x0, local copies, waits for them, and re-layouts: 2.32 us -> none  [on_device(): 3.4445 * iterate]
  transfers between devices with their start and end apart: 0 -> 7, of which waited for: 0 -> 7; matrix products, arithmetic and copies ran while one was open for 0% -> 0% of each run, Pallas kernels for 0% -> 0%
where the time goes in v1:
time: 158 us; the launch traced here: 157 us
  waiting for transfers between devices  67.8 us (43%)
  blocking collectives  51.9 us (33%)
  matrix products  13.6 us (9%)
  starting transfers between devices  10.8 us (7%)
  other arithmetic  6.32 us (4%)
  local copies, waits for them, and re-layouts  5.95 us (4%)
    all_to_all x1, blocking collectives, on_device(): back = lax.all_to_all(x, 'shard', split_axis=1, concat_axis=0, tiled=True)  51.9 us
    all_to_all x1, waiting for transfers between devices, on_device(): lax.all_to_all(new_momentum, 'shard', split_axis=0, concat_axis=1, tiled=...  48.2 us
    ppermute x2, waiting for transfers between devices, summed_over_model(): lax.ppermute(own, 'model', [(i, i ^ dist) for i in range(model)])  13.6 us
    dot_general x16, matrix products, mm(): return jnp.einsum('mij,mjk->mik', a, b, precision=HI)  9.47 us
    all_to_all x1, starting transfers between devices, on_device(): lax.all_to_all(new_momentum, 'shard', split_axis=0, concat_axis=1, tiled=...  7.28 us
    add x1, other arithmetic, on_device(): new_momentum = hold_rate * moment_stack + grad_stack  4.24 us
    dot_general x2, matrix products, gram_of(): return jnp.einsum('mik,mjk->mij', x, x, precision=HI)  4.13 us
  transfers between devices with their start and end apart: 7, of which 7 were waited for; matrix products, arithmetic and copies ran while one was open for 0% of the time, Pallas kernels for 0%

profile of v1, /device:TPU:0, one launch (start us, length us, event | category | flops | bytes accessed | tf_op | source)
XLA Modules:
  0.0 157.3 jit_solution(1436535767304604527)
XLA Ops:
  0.6 4.2 %multiply_add_fusion = f32[64,16,512]{2,1,0:T(8,128)} fusion(f32[64,16,512]{2,1,0:T(8,128)} %param.3, f32[64,16,512]{2,1,0:T(8,128)} %param.4), kind=kLoop, calls=%fused_computation.1 | loop fusion | flops 1048576 | bytes 6291456 | tf_op jit(solution)/shard_map/add | solution.py:70
  4.9 7.3 %all-to-all-start = ((f32[64,16,512]{2,1,0:T(8,128)}), f32[64,16,512]{2,1,0:T(8,128)S(1)}, u32[]{:S(2)}, u32[]{:S(2)}) async-start(f32[64,16,512]{2,1,0:T(8,128)} %multiply_add_fusion), calls=%async_computation | async-start | bytes 4194304 | tf_op jit(solution)/shard_map/all_to_all | solution.py:72
  12.2 48.2 %all-to-all-done = f32[64,16,512]{2,1,0:T(8,128)S(1)} async-done(((f32[64,16,512]{2,1,0:T(8,128)}), f32[64,16,512]{2,1,0:T(8,128)S(1)}, u32[]{:S(2)}, u32[]{:S(2)}) %all-to-all-start) | async-done | bytes 2097184 | tf_op jit(solution)/shard_map/all_to_all | solution.py:72
  60.4 0.0 copy-start
  60.4 1.3 copy-done
  61.7 1.8 %copy.7 = f32[8,8,16,512]{3,2,0,1:T(8,128)S(1)} copy(f32[8,8,16,512]{3,2,1,0:T(8,128)} %bitcast.42) | data formatting | bytes 4194304 | tf_op jit(solution)/shard_map/all_to_all | solution.py:72
  63.5 2.1 %fusion.28 = f32[8,128,128]{2,1,0:T(8,128)S(1)} fusion(f32[8,128,512]{2,1,0:T(8,128)S(1)} %bitcast.40), kind=kOutput, calls=%fused_computation.46 | convolution fusion | flops 805306368 | bytes 2621440 | tf_op jit(solution)/shard_map/mik,mjk->mij/dot_general | solution.py:18
  65.6 0.1 collective-permute-start
  65.7 1.5 collective-permute-done
  67.2 1.6 %collective-permute-start.1 = (f32[4,128,128]{2,1,0:T(8,128)S(1)}, f32[4,128,128]{2,1,0:T(8,128)S(1)}, u32[]{:S(2)}, u32[]{:S(2)}) collective-permute-start(f32[4,128,128]{2,1,0:T(8,128)S(1)} %dynamic-slice_add_fusion.1), channel_id=1, source_target_pairs={{0,2},{1,3},{2,0},{3,1},{4,6},{5,7},{6,4},{7,5},{8,10},{9,11},{10,... | collective-permute-start | bytes 786440 | tf_op jit(solution)/shard_map/ppermute | solution.py:43
  68.8 6.8 %collective-permute-done.1 = f32[4,128,128]{2,1,0:T(8,128)S(1)} collective-permute-done((f32[4,128,128]{2,1,0:T(8,128)S(1)}, f32[4,128,128]{2,1,0:T(8,128)S(1)}, u32[]{:S(2)}, u32[]{:S(2)}) %collective-permute-start.1) | collective-permute-done | bytes 262176 | tf_op jit(solution)/shard_map/ppermute | solution.py:43
  75.6 0.1 select_reduce_fusion
  75.8 0.5 add_add_fusion.1
  76.3 0.4 fusion.17
  76.7 0.4 fusion.29
  77.1 0.4 fusion.2
  77.5 0.4 convolution_multiply_fusion.3
  77.9 0.1 collective-permute-start.2
  78.0 1.5 collective-permute-done.2
  79.5 1.8 %fusion.3 = f32[8,128,512]{2,1,0:T(8,128)S(1)} fusion(f32[8,128,512]{2,1,0:T(8,128)S(1)} %bitcast.41, f32[4,128,128]{2,1,0:T(8,128)S(1)} %collective-permute-done.2, f32[4,128,128]{2,1,0:T(8,128)S(1)} %convolution_multiply_fusion.3, pred[]{:T(512)S(6)} %eq.27), kind=kOutput, calls=%fused_computation.12 | convolution fusion | flops 805699584 | bytes 4718593 | tf_op jit(solution)/shard_map/mij,mjk->mik/dot_general | solution.py:14
  81.4 2.1 %fusion.30 = f32[8,128,128]{2,1,0:T(8,128)S(1)} fusion(f32[8,128,512]{2,1,0:T(8,128)S(1)} %fusion.3), kind=kOutput, calls=%fused_computation.48 | convolution fusion | flops 805306368 | bytes 2621440 | tf_op jit(solution)/shard_map/mik,mjk->mij/dot_general | solution.py:18
  83.5 0.2 collective-permute-start.3
  83.7 1.4 collective-permute-done.3
  85.1 1.6 %collective-permute-start.4 = (f32[4,128,128]{2,1,0:T(8,128)S(1)}, f32[4,128,128]{2,1,0:T(8,128)S(1)}, u32[]{:S(2)}, u32[]{:S(2)}) collective-permute-start(f32[4,128,128]{2,1,0:T(8,128)S(1)} %dynamic-slice_add_fusion), channel_id=1, source_target_pairs={{0,2},{1,3},{2,0},{3,1},{4,6},{5,7},{6,4},{7,5},{8,10},{9,11},{10,... | collective-permute-start | bytes 786440 | tf_op jit(solution)/shard_map/ppermute | solution.py:43
  86.7 6.8 %collective-permute-done.4 = f32[4,128,128]{2,1,0:T(8,128)S(1)} collective-permute-done((f32[4,128,128]{2,1,0:T(8,128)S(1)}, f32[4,128,128]{2,1,0:T(8,128)S(1)}, u32[]{:S(2)}, u32[]{:S(2)}) %collective-permute-start.4) | collective-permute-done | bytes 262176 | tf_op jit(solution)/shard_map/ppermute | solution.py:43
  93.6 0.4 add_add_fusion
  93.9 0.4 fusion.31
  94.4 0.4 fusion.32
  94.8 0.4 fusion.1
  95.1 0.4 fusion.35
  95.5 0.4 fusion.33
  95.9 0.4 fusion.34
  96.3 0.4 fusion
  96.7 0.4 fusion.36
  97.1 0.1 collective-permute-start.5
  97.2 1.5 collective-permute-done.5
  98.7 2.0 %fusion.9 = f32[8,128,512]{2,1,0:T(8,128)S(1)} fusion(f32[8,128,512]{2,1,0:T(8,128)S(1)} %fusion.3, f32[4,128,128]{2,1,0:T(8,128)S(1)} %collective-permute-done.5, f32[4,128,128]{2,1,0:T(8,128)S(1)} %fusion.36, pred[]{:T(512)S(6)} %eq.27), kind=kOutput, calls=%fused_computation.19 | convolution fusion | flops 805699584 | bytes 4718593 | tf_op jit(solution)/shard_map/mij,mjk->mik/dot_general | solution.py:14
  100.8 1.2 copy.8
  102.0 51.9 %all_to_all.36 = f32[8,128,512]{2,0,1:T(8,128)S(1)} all-to-all(f32[8,128,512]{2,0,1:T(8,128)S(1)} %copy.8), channel_id=1, replica_groups=mesh['shard'=8,'model'=4] {'shard'}, dimensions={1} | all-to-all | bytes 4194304 | tf_op jit(solution)/shard_map/all_to_all | solution.py:74
  153.9 0.0 copy-start.1
  153.9 1.2 copy.9
  155.1 0.4 copy-done.1
  155.5 1.8 %bitcast_subtract_fusion = f32[64,16,512]{2,1,0:T(8,128)} fusion(f32[8,8,16,512]{3,2,1,0:T(8,128)S(1)} %copy.9, f32[64,16,512]{2,1,0:T(8,128)S(1)} %copy-done.1), kind=kLoop, calls=%fused_computation | loop fusion | flops 1048576 | bytes 6291456 | tf_op jit(solution)/shard_map/sub | solution.py:75
  (8 shorter events, 0.2 us)
Async XLA Ops:
  4.9 55.5 %all-to-all-start = ((f32[64,16,512]{2,1,0:T(8,128)}), f32[64,16,512]{2,1,0:T(8,128)S(1)}, u32[]{:S(2)}, u32[]{:S(2)}) async-start(f32[64,16,512]{2,1,0:T(8,128)} %multiply_add_fusion), calls=%async_computation | async-start | bytes 4194304 | tf_op jit(solution)/shard_map/all_to_all | solution.py:72
  60.4 1.3 copy-start
  65.6 1.6 %collective-permute-start = (f32[4,128,128]{2,1,0:T(8,128)S(1)}, f32[4,128,128]{2,1,0:T(8,128)S(1)}, u32[]{:S(2)}, u32[]{:S(2)}) collective-permute-start(f32[4,128,128]{2,1,0:T(8,128)S(1)} %constant_dynamic-slice_fusion.1), channel_id=1, source_target_pairs={{0,1},{1,0},{2,3},{3,2},{4,5},{5,4},{6,7},{7,6},{8,9},{9,8},{10,11... | collective-permute-start | bytes 786440 | tf_op jit(solution)/shard_map/ppermute | solution.py:40
  67.2 8.4 %collective-permute-start.1 = (f32[4,128,128]{2,1,0:T(8,128)S(1)}, f32[4,128,128]{2,1,0:T(8,128)S(1)}, u32[]{:S(2)}, u32[]{:S(2)}) collective-permute-start(f32[4,128,128]{2,1,0:T(8,128)S(1)} %dynamic-slice_add_fusion.1), channel_id=1, source_target_pairs={{0,2},{1,3},{2,0},{3,1},{4,6},{5,7},{6,4},{7,5},{8,10},{9,11},{10,... | collective-permute-start | bytes 786440 | tf_op jit(solution)/shard_map/ppermute | solution.py:43
  77.9 1.6 %collective-permute-start.2 = (f32[4,128,128]{2,1,0:T(8,128)S(1)}, f32[4,128,128]{2,1,0:T(8,128)S(1)}, u32[]{:S(2)}, u32[]{:S(2)}) collective-permute-start(f32[4,128,128]{2,1,0:T(8,128)S(1)} %convolution_multiply_fusion.3), channel_id=1, source_target_pairs={{0,1},{1,0},{2,3},{3,2},{4,5},{5,4},{6,7},{7,6},{8,9},{9,8},{10,11... | collective-permute-start | bytes 786440 | tf_op jit(solution)/shard_map/ppermute | solution.py:50
  83.5 1.6 %collective-permute-start.3 = (f32[4,128,128]{2,1,0:T(8,128)S(1)}, f32[4,128,128]{2,1,0:T(8,128)S(1)}, u32[]{:S(2)}, u32[]{:S(2)}) collective-permute-start(f32[4,128,128]{2,1,0:T(8,128)S(1)} %constant_dynamic-slice_fusion), channel_id=1, source_target_pairs={{0,1},{1,0},{2,3},{3,2},{4,5},{5,4},{6,7},{7,6},{8,9},{9,8},{10,11... | collective-permute-start | bytes 786440 | tf_op jit(solution)/shard_map/ppermute | solution.py:40
  85.1 8.4 %collective-permute-start.4 = (f32[4,128,128]{2,1,0:T(8,128)S(1)}, f32[4,128,128]{2,1,0:T(8,128)S(1)}, u32[]{:S(2)}, u32[]{:S(2)}) collective-permute-start(f32[4,128,128]{2,1,0:T(8,128)S(1)} %dynamic-slice_add_fusion), channel_id=1, source_target_pairs={{0,2},{1,3},{2,0},{3,1},{4,6},{5,7},{6,4},{7,5},{8,10},{9,11},{10,... | collective-permute-start | bytes 786440 | tf_op jit(solution)/shard_map/ppermute | solution.py:43
  97.1 1.6 %collective-permute-start.5 = (f32[4,128,128]{2,1,0:T(8,128)S(1)}, f32[4,128,128]{2,1,0:T(8,128)S(1)}, u32[]{:S(2)}, u32[]{:S(2)}) collective-permute-start(f32[4,128,128]{2,1,0:T(8,128)S(1)} %fusion.36), channel_id=1, source_target_pairs={{0,1},{1,0},{2,3},{3,2},{4,5},{5,4},{6,7},{7,6},{8,9},{9,8},{10,11... | collective-permute-start | bytes 786440 | tf_op jit(solution)/shard_map/ppermute | solution.py:50
  153.9 1.6 %copy-start.1 = (f32[64,16,512]{2,1,0:T(8,128)S(1)}, f32[64,16,512]{2,1,0:T(8,128)}, u32[]{:S(2)}) copy-start(f32[64,16,512]{2,1,0:T(8,128)} %param.5) | copy-start | bytes 6291460

commit v2 on v0

v2 whole, which is shorter than its diff:
```python
import jax
import jax.numpy as jnp
from jax import lax
from jax.sharding import PartitionSpec as P


ITERS = 5
hold_rate = 0.95
learn_rate = 1.0
decay_rate = 0.1
HI = lax.Precision.HIGHEST
AXES = ("shard", "model")


def orthogonal(whole):
    norm = lax.rsqrt(jnp.sum(whole * whole, axis=(1, 2), keepdims=True) + 1e-06)
    iterate = whole * norm
    for _ in range(ITERS):
        gram = jnp.einsum("mik,mjk->mij", iterate, iterate, precision=HI)
        mixed = -4.775 * gram + 2.0315 * jnp.einsum("mij,mjk->mik", gram, gram, precision=HI)
        iterate = 3.4445 * iterate + jnp.einsum("mij,mjk->mik", mixed, iterate, precision=HI)
    return iterate


def make(mesh):
    shards, model = mesh.shape["shard"], mesh.shape["model"]
    devices = shards * model

    def on_device(grad_stack, moment_stack, weight_stack):
        new_momentum = hold_rate * moment_stack + grad_stack
        mats, rows, cols = new_momentum.shape
        each = mats // devices
        pieces = 2 if each % 2 == 0 else 1
        w = each // pieces
        split = new_momentum.reshape(devices, each, rows, cols)
        kept = ((1.0 - learn_rate * decay_rate) * weight_stack).reshape(split.shape)
        arrived = []
        for c in range(pieces):
            arrived.append(lax.all_to_all(split[:, c * w:(c + 1) * w], AXES, split_axis=0, concat_axis=0, tiled=True))
        backs = []
        for c in range(pieces):
            x = arrived[c].reshape(shards, model, w, rows, cols).transpose(2, 0, 3, 1, 4)
            x = orthogonal(x.reshape(w, shards * rows, model * cols))
            x = x.reshape(w, shards, rows, model, cols).transpose(1, 3, 0, 2, 4).reshape(devices, w, rows, cols)
            if c + 1 < pieces:
                x, arrived[c + 1] = lax.optimization_barrier((x, arrived[c + 1]))
            backs.append(lax.all_to_all(x, AXES, split_axis=0, concat_axis=0, tiled=True))
        new_weights = kept - learn_rate * jnp.concatenate(backs, axis=1)
        return (new_weights.reshape(mats, rows, cols), new_momentum)

    return on_device


def solution(mesh):
    spec = P(None, "shard", "model")
    return jax.shard_map(
        make(mesh), mesh=mesh, in_specs=(spec,) * 3, out_specs=(spec,) * 2, check_vma=False
    )
```

time: 202 us -> 133 us (0.66)
  blocking collectives: 164 us -> 62.9 us
  waiting for transfers between devices: 0 us -> 20.5 us
  starting transfers between devices: 0 us -> 7.25 us
  other arithmetic: 4.91 us -> 7.03 us
    all_to_all x4 -> x2, blocking collectives: 164 us -> 62.9 us  [the longest x1 33.3 us: on_device(): lax.all_to_all(split[:, c * w:(c + 1) * w], AXES, split_axis=0, concat_ax...]
    all_to_all x0 -> x2, waiting for transfers between devices: none -> 20.5 us  [the longest x1 11.6 us: on_device(): lax.all_to_all(x, AXES, split_axis=0, concat_axis=0, tiled=True)]
    all_to_all x0 -> x2, starting transfers between devices: none -> 7.25 us  [the longest x1 3.63 us: on_device(): lax.all_to_all(x, AXES, split_axis=0, concat_axis=0, tiled=True)]
    all_to_all x6 -> x0, local copies, waits for them, and re-layouts: 6.36 us -> none  [the longest x3 4.76 us: on_device(): lax.all_to_all(iterate, 'model', split_axis=2, concat_axis=0, tiled=True)]
    reshape x0 -> x4, local copies, waits for them, and re-layouts: none -> 3.02 us  [on_device(): x.reshape(w, shards, rows, model, cols).transpose(1, 3, 0, 2, 4)]
    unnamed x4 -> x8, local copies, waits for them, and re-layouts: 0.4 us -> 3.13 us
    mul x0 -> x4, local copies, waits for them, and re-layouts: none -> 2.72 us  [the longest x2 1.36 us: orthogonal(): 3.4445 * iterate + jnp.einsum('mij,mjk->mik', mixed, iterate, precision=HI)]
    add x1 -> x0, local copies, waits for them, and re-layouts: 2.32 us -> none  [on_device(): 3.4445 * iterate]
  transfers between devices with their start and end apart: 0 -> 2, of which waited for: 0 -> 2; matrix products, arithmetic and copies ran while one was open for 0% -> 23% of each run, Pallas kernels for 0% -> 0%
where the time goes in v2:
time: 133 us
  blocking collectives  62.9 us (47%)
  matrix products  22.4 us (17%)
  waiting for transfers between devices  20.5 us (15%)
  local copies, waits for them, and re-layouts  10.2 us (8%)
  starting transfers between devices  7.25 us (5%)
  other arithmetic  7.03 us (5%)
  between operations  2.32 us (2%)
    all_to_all x1, blocking collectives, on_device(): lax.all_to_all(split[:, c * w:(c + 1) * w], AXES, split_axis=0, concat_ax...  33.3 us
    all_to_all x1, blocking collectives, on_device(): lax.all_to_all(x, AXES, split_axis=0, concat_axis=0, tiled=True)  29.6 us
    all_to_all x1, waiting for transfers between devices, on_device(): lax.all_to_all(x, AXES, split_axis=0, concat_axis=0, tiled=True)  11.6 us
    dot_general x10, matrix products, orthogonal(): jnp.einsum('mij,mjk->mik', mixed, iterate, precision=HI)  10.5 us
    dot_general x10, matrix products, orthogonal(): gram = jnp.einsum('mik,mjk->mij', iterate, iterate, precision=HI)  9.84 us
    all_to_all x1, waiting for transfers between devices, on_device(): lax.all_to_all(split[:, c * w:(c + 1) * w], AXES, split_axis=0, concat_ax...  8.9 us
    all_to_all x1, starting transfers between devices, on_device(): lax.all_to_all(x, AXES, split_axis=0, concat_axis=0, tiled=True)  3.63 us
    all_to_all x1, starting transfers between devices, on_device(): lax.all_to_all(split[:, c * w:(c + 1) * w], AXES, split_axis=0, concat_ax...  3.62 us
  transfers between devices with their start and end apart: 2, of which 2 were waited for; matrix products, arithmetic and copies ran while one was open for 23% of the time, Pallas kernels for 0%

profile of v2, /device:TPU:0, one launch (start us, length us, event | category | flops | bytes accessed | tf_op | source)
XLA Modules:
  0.0 132.6 jit_solution(7167163401922682552)
XLA Ops:
  0.6 2.7 %multiply_add_fusion = f32[64,16,512]{2,1,0:T(8,128)S(1)} fusion(f32[64,16,512]{2,1,0:T(8,128)} %param.3, f32[64,16,512]{2,1,0:T(8,128)} %param.4), kind=kLoop, calls=%fused_computation.12 | loop fusion | flops 1048576 | bytes 6291456 | tf_op jit(solution)/shard_map/add | solution.py:30
  3.3 0.0 copy-start
  3.4 1.3 fusion.10
  4.7 0.3 copy-done
  5.0 33.3 %all_to_all.20 = f32[32,1,16,512]{3,2,1,0:T(8,128)S(1)} all-to-all(f32[32,1,16,512]{3,2,1,0:T(8,128)S(1)} %get-tuple-element.11), channel_id=1, replica_groups=mesh['shard'=8,'model'=4] {'shard','model'}, dimensions={0} | all-to-all | bytes 2097152 | tf_op jit(solution)/shard_map/all_to_all | solution.py:39
  38.3 3.6 %all-to-all-start.1 = ((f32[32,1,16,512]{3,2,1,0:T(8,128)}), f32[32,1,16,512]{3,2,1,0:T(8,128)S(1)}, u32[]{:S(2)}, u32[]{:S(2)}) async-start(f32[32,1,16,512]{3,2,1,0:T(8,128)} %get-tuple-element.10), calls=%async_computation.1 | async-start | bytes 2097152 | tf_op jit(solution)/shard_map/all_to_all | solution.py:39
  42.0 0.9 multiply_reduce_fusion.1
  43.5 0.3 broadcast_multiply_fusion.2
  43.8 0.7 copy.18
  44.5 0.3 copy.26
  44.8 0.7 copy.19
  45.5 0.3 copy.27
  45.9 1.0 fusion.11
  46.9 0.2 fusion.9
  47.1 1.0 convolution_add_fusion.9
  48.1 1.0 fusion.12
  49.1 0.2 fusion.8
  49.3 1.0 convolution_add_fusion.8
  50.3 1.0 fusion.13
  51.3 0.2 fusion.7
  51.5 1.0 convolution_add_fusion.7
  52.6 1.0 fusion.14
  53.6 0.2 fusion.6
  53.8 1.0 convolution_add_fusion.6
  54.8 1.0 fusion.15
  55.8 0.2 fusion.5
  56.0 1.2 convolution_add_fusion.5
  57.3 0.7 reshape.285
  58.0 1.3 copy.20
  59.3 8.9 %all-to-all-done.1 = f32[32,1,16,512]{3,2,1,0:T(8,128)S(1)} async-done(((f32[32,1,16,512]{3,2,1,0:T(8,128)}), f32[32,1,16,512]{3,2,1,0:T(8,128)S(1)}, u32[]{:S(2)}, u32[]{:S(2)}) %all-to-all-start.1) | async-done | bytes 1048608 | tf_op jit(solution)/shard_map/all_to_all | solution.py:39
  68.2 0.9 multiply_reduce_fusion
  69.7 3.6 %all-to-all-start.2 = ((f32[32,1,16,512]{3,2,1,0:T(8,128)}), f32[32,1,16,512]{3,2,1,0:T(8,128)S(1)}, u32[]{:S(2)}, u32[]{:S(2)}) async-start(f32[32,1,16,512]{3,2,1,0:T(8,128)} %bitcast.7), calls=%async_computation.2 | async-start | bytes 2097152 | tf_op jit(solution)/shard_map/all_to_all | solution.py:47
  73.4 0.3 broadcast_multiply_fusion.1
  73.7 0.7 copy.22
  74.3 0.3 copy.28
  74.7 0.7 copy.23
  75.4 0.3 copy.29
  75.7 1.0 fusion.16
  76.7 0.2 fusion.4
  76.9 1.0 convolution_add_fusion.4
  78.0 1.0 fusion.17
  78.9 0.2 fusion.3
  79.2 1.0 convolution_add_fusion.3
  80.2 1.0 fusion.18
  81.2 0.2 fusion.2
  81.4 1.0 convolution_add_fusion.2
  82.4 1.0 fusion.19
  83.4 0.2 fusion.1
  83.6 1.0 convolution_add_fusion.1
  84.7 1.0 fusion.20
  85.7 0.2 fusion
  85.9 1.0 convolution_add_fusion
  86.9 0.7 reshape.287
  87.6 0.3 copy.24
  88.0 11.6 %all-to-all-done.2 = f32[32,1,16,512]{3,2,1,0:T(8,128)S(1)} async-done(((f32[32,1,16,512]{3,2,1,0:T(8,128)}), f32[32,1,16,512]{3,2,1,0:T(8,128)S(1)}, u32[]{:S(2)}, u32[]{:S(2)}) %all-to-all-start.2) | async-done | bytes 1048608 | tf_op jit(solution)/shard_map/all_to_all | solution.py:47
  99.6 29.6 %all_to_all.21 = f32[32,1,16,512]{3,2,1,0:T(8,128)S(1)} all-to-all(f32[32,1,16,512]{3,2,1,0:T(8,128)S(1)} %bitcast.103), channel_id=1, replica_groups=mesh['shard'=8,'model'=4] {'shard','model'}, dimensions={0} | all-to-all | bytes 2097152 | tf_op jit(solution)/shard_map/all_to_all | solution.py:47
  129.2 0.0 copy-start.1
  129.2 0.2 pad_maximum_fusion
  129.4 1.4 %copy-done.1 = f32[64,16,512]{2,1,0:T(8,128)S(1)} copy-done((f32[64,16,512]{2,1,0:T(8,128)S(1)}, f32[64,16,512]{2,1,0:T(8,128)}, u32[]{:S(2)}) %copy-start.1) | copy-done | bytes 2097176
  130.8 1.8 %bitcast_subtract_fusion = f32[64,16,512]{2,1,0:T(8,128)} fusion(f32[32,2,16,512]{3,2,1,0:T(8,128)S(1)} %pad_maximum_fusion, f32[64,16,512]{2,1,0:T(8,128)S(1)} %copy-done.1), kind=kLoop, calls=%fused_computation.11 | loop fusion | flops 1048576 | bytes 6291456 | tf_op jit(solution)/shard_map/sub | solution.py:48
Async XLA Ops:
  3.3 1.7 %copy-start = (f32[64,16,512]{2,1,0:T(8,128)}, f32[64,16,512]{2,1,0:T(8,128)S(1)}, u32[]{:S(2)}) copy-start(f32[64,16,512]{2,1,0:T(8,128)S(1)} %multiply_add_fusion) | copy-start | bytes 6291460
  38.3 29.8 %all-to-all-start.1 = ((f32[32,1,16,512]{3,2,1,0:T(8,128)}), f32[32,1,16,512]{3,2,1,0:T(8,128)S(1)}, u32[]{:S(2)}, u32[]{:S(2)}) async-start(f32[32,1,16,512]{3,2,1,0:T(8,128)} %get-tuple-element.10), calls=%async_computation.1 | async-start | bytes 2097152 | tf_op jit(solution)/shard_map/all_to_all | solution.py:39
  69.7 29.8 %all-to-all-start.2 = ((f32[32,1,16,512]{3,2,1,0:T(8,128)}), f32[32,1,16,512]{3,2,1,0:T(8,128)S(1)}, u32[]{:S(2)}, u32[]{:S(2)}) async-start(f32[32,1,16,512]{3,2,1,0:T(8,128)} %bitcast.7), calls=%async_computation.2 | async-start | bytes 2097152 | tf_op jit(solution)/shard_map/all_to_all | solution.py:47
  129.2 1.6 %copy-start.1 = (f32[64,16,512]{2,1,0:T(8,128)S(1)}, f32[64,16,512]{2,1,0:T(8,128)}, u32[]{:S(2)}) copy-start(f32[64,16,512]{2,1,0:T(8,128)} %param.5) | copy-start | bytes 6291460

commit v3 on v1

v3 whole, which is shorter than its diff:
```python
import functools

import jax
import jax.numpy as jnp
from jax import lax
from jax.experimental import pallas as pl
from jax.experimental.pallas import tpu as pltpu
from jax.sharding import PartitionSpec as P


ITERS = 5
EARLY = 2
hold_rate = 0.95
learn_rate = 1.0
decay_rate = 0.1
A0, A1, A2 = 3.4445, -4.775, 2.0315
HI = lax.Precision.HIGHEST
AXES = ("shard", "model")
F32 = jnp.float32
VMEM = pl.BlockSpec(memory_space=pltpu.VMEM)


def dot(a, b):
    return lax.dot_general(a, b, (((1,), (0,)), ((), ())), precision=HI, preferred_element_type=F32)


def dot_t(a, b):
    return lax.dot_general(a, b, (((1,), (1,)), ((), ())), precision=HI, preferred_element_type=F32)


def eye_of(n):
    i = lax.broadcasted_iota(jnp.int32, (n, n), 0)
    j = lax.broadcasted_iota(jnp.int32, (n, n), 1)
    return (i == j).astype(F32)


def chain(grams, steps, eye):
    totals = None
    for step in range(steps):
        squares = [dot(g, g) for g in grams]
        ps = [A0 * eye + A1 * g + A2 * s for g, s in zip(grams, squares)]
        if step < steps - 1:
            halves = [dot(p, g) for p, g in zip(ps, grams)]
        totals = ps if totals is None else [dot(p, t) for p, t in zip(ps, totals)]
        if step < steps - 1:
            grams = [dot(h, p) for h, p in zip(halves, ps)]
    return totals


def inverse_norm(gram, eye):
    return lax.rsqrt(jnp.sum(gram * eye, axis=(0, 1), keepdims=True) + 1e-06)


def whole_kernel(shards, model, rows, cols, x_ref, o_ref, a_ref):
    eye = eye_of(shards * rows)

    def load(s, _):
        for m in range(model):
            a_ref[pl.ds(pl.multiple_of(s * rows, rows), rows), m * cols:(m + 1) * cols] = x_ref[s * model + m]
        return 0

    lax.fori_loop(0, shards, load, 0)

    def gram(m, total):
        at = pl.ds(pl.multiple_of(m * cols, cols), cols)
        return total + dot_t(a_ref[:, at], a_ref[:, at])

    zero = jnp.zeros(eye.shape, F32)
    g = lax.fori_loop(0, model, gram, zero)
    norm = inverse_norm(g, eye)
    q = chain([g * (norm * norm)], EARLY, eye)[0] * norm

    def early(m, total):
        at = pl.ds(pl.multiple_of(m * cols, cols), cols)
        y = dot(q, a_ref[:, at])
        a_ref[:, at] = y
        return total + dot_t(y, y)

    g = lax.fori_loop(0, model, early, zero)
    r = chain([g], ITERS - EARLY, eye)[0]

    def late(m, _):
        y = dot(r, a_ref[:, pl.ds(pl.multiple_of(m * cols, cols), cols)])
        for s in range(shards):
            o_ref[s * model + m] = y[s * rows:(s + 1) * rows]
        return 0

    lax.fori_loop(0, model, late, 0)


def whole(x, shards, model):
    _, rows, cols = x.shape
    flops = 8 * (shards * rows) ** 2 * model * cols * 6
    return pl.pallas_call(
        functools.partial(whole_kernel, shards, model, rows, cols),
        out_shape=jax.ShapeDtypeStruct(x.shape, F32),
        in_specs=[VMEM],
        out_specs=VMEM,
        scratch_shapes=[pltpu.VMEM((shards * rows, model * cols), F32)],
        cost_estimate=pl.CostEstimate(flops=flops, bytes_accessed=8 * x.size, transcendentals=0),
    )(x)


def mm(a, b):
    return jnp.einsum("mij,mjk->mik", a, b, precision=HI)


def gram_of(x):
    return jnp.einsum("mik,mjk->mij", x, x, precision=HI)


def stacked_chain(g, steps, eye):
    total = None
    for step in range(steps):
        p = A0 * eye + A1 * g + A2 * mm(g, g)
        total = p if total is None else mm(p, total)
        if step < steps - 1:
            g = mm(mm(p, g), p)
    return total


def swap(x, axis, size, bits):
    return lax.ppermute(x, axis, [(i, i ^ bits) for i in range(size)])


def summed(g, model):
    half = g.shape[0] // 2
    bit = lax.axis_index("model") % 2
    own = lax.dynamic_slice_in_dim(g, bit * half, half, 0)
    send = lax.dynamic_slice_in_dim(g, (1 - bit) * half, half, 0)
    own = own + swap(send, "model", model, 1)
    return own + swap(own, "model", model, 2)


def joined(own, model):
    bit = lax.axis_index("model") % 2
    other = swap(own, "model", model, 1)
    return jnp.where(bit == 0, jnp.concatenate([own, other]), jnp.concatenate([other, own]))


def spread(x, model):
    eye = jnp.eye(x.shape[1], dtype=F32)
    g = gram_of(x)
    g = summed(g, model)
    r = lax.rsqrt(jnp.einsum("mii->m", g) + 1e-06)[:, None, None]
    q = stacked_chain(g * (r * r), EARLY, eye) * r
    x = mm(joined(q, model), x)
    g = summed(gram_of(x), model)
    q = joined(stacked_chain(g, ITERS - EARLY, eye), model)
    return mm(q, x)


def direct(blocks, shards):
    return [blocks[0]] + [swap(blocks[d], "shard", shards, d) for d in range(1, shards)]


def mixed(shards, model, grad_stack, moment_stack, weight_stack):
    mats, rows, cols = grad_stack.shape
    each = mats // shards
    w = each // 2
    me = lax.axis_index("shard")
    cut = (shards, each, rows, cols)
    first = hold_rate * moment_stack.reshape(cut)[:, :w] + grad_stack.reshape(cut)[:, :w]
    first, grad_stack = lax.optimization_barrier((first, grad_stack))
    new_momentum = hold_rate * moment_stack + grad_stack
    split = new_momentum.reshape(cut)
    first = lax.all_to_all(first.reshape(shards * model, rows, cols), AXES, split_axis=0, concat_axis=0, tiled=True)
    second = [lax.dynamic_slice(split, (me ^ d, w, 0, 0), (1, w, rows, cols))[0] for d in range(shards)]
    second = direct(second, shards)

    first = whole(first, shards, model)
    first = lax.all_to_all(first, AXES, split_axis=0, concat_axis=0, tiled=True)

    x = jnp.concatenate([b[None] for b in second], axis=0).transpose(1, 0, 2, 3)
    x = spread(x.reshape(w, shards * rows, cols), model).reshape(w, shards, rows, cols)
    second = [x[:, d] for d in range(shards)]
    second = direct(second, shards)

    kept = lax.optimization_barrier((1.0 - learn_rate * decay_rate) * weight_stack.reshape(cut))
    total = kept.at[:, :w].add(-learn_rate * first.reshape(shards, w, rows, cols))
    for d in range(shards):
        at = (me ^ d, w, 0, 0)
        total = lax.dynamic_update_slice(
            total, lax.dynamic_slice(total, at, (1, w, rows, cols)) - learn_rate * second[d][None], at
        )
    return (total.reshape(mats, rows, cols), new_momentum)


def orthogonal(whole):
    iterate = whole * lax.rsqrt(jnp.sum(whole * whole, axis=(1, 2), keepdims=True) + 1e-06)
    for _ in range(ITERS):
        gram = jnp.einsum("mik,mjk->mij", iterate, iterate, precision=HI)
        mix = A1 * gram + A2 * jnp.einsum("mij,mjk->mik", gram, gram, precision=HI)
        iterate = A0 * iterate + jnp.einsum("mij,mjk->mik", mix, iterate, precision=HI)
    return iterate


def plain(shards, model, grad_stack, moment_stack, weight_stack):
    new_momentum = hold_rate * moment_stack + grad_stack
    mats, rows, cols = new_momentum.shape
    x = lax.all_to_all(new_momentum, AXES, split_axis=0, concat_axis=0, tiled=True)
    x = x.reshape(shards, model, -1, rows, cols).transpose(2, 0, 3, 1, 4)
    x = orthogonal(x.reshape(-1, shards * rows, model * cols))
    x = x.reshape(-1, shards, rows, model, cols).transpose(1, 3, 0, 2, 4).reshape(mats, rows, cols)
    x = lax.all_to_all(x, AXES, split_axis=0, concat_axis=0, tiled=True)
    return ((1.0 - learn_rate * decay_rate) * weight_stack - learn_rate * x, new_momentum)


def solution(mesh):
    shards, model = mesh.shape["shard"], mesh.shape["model"]
    spec = P(None, "shard", "model")
    use = mixed if shards == 8 and model == 4 else plain
    return jax.shard_map(
        functools.partial(use, shards, model),
        mesh=mesh, in_specs=(spec,) * 3, out_specs=(spec,) * 2, check_vma=False,
    )
```

time: 158 us -> 137 us (0.87); the launches traced: 157 us -> 134 us
  blocking collectives: 51.9 us -> 0 us
  starting transfers between devices: 10.8 us -> 43.2 us
  waiting for transfers between devices: 67.8 us -> 55.4 us
  Pallas kernels: 0 us -> 11.1 us
  matrix products: 13.6 us -> 8.08 us
  other arithmetic: 6.32 us -> 10.5 us
    all_to_all x1 -> x0, blocking collectives: 51.9 us -> none  [on_device(): back = lax.all_to_all(x, 'shard', split_axis=1, concat_axis=0, tiled=True)]
    all_to_all x1 -> x2, waiting for transfers between devices: 48.2 us -> 14.2 us  [the longest x1 14.2 us: mixed(): first = lax.all_to_all(first, AXES, split_axis=0, concat_axis=0, tiled=True)]
    ppermute x6 -> x20, starting transfers between devices: 3.57 us -> 30.6 us  [swap(): return lax.ppermute(x, axis, [(i, i ^ bits) for i in range(size)])]
    ppermute x6 -> x20, waiting for transfers between devices: 19.6 us -> 41.2 us  [swap(): return lax.ppermute(x, axis, [(i, i ^ bits) for i in range(size)])]
    pallas_call x0 -> x1, Pallas kernels: none -> 11.1 us  [whole(): pl.pallas_call(functools.partial(whole_kernel, shards, model, rows, cols)...]
    all_to_all x1 -> x2, starting transfers between devices: 7.28 us -> 12.6 us  [the longest x1 8.11 us: mixed(): lax.all_to_all(first.reshape(shards * model, rows, cols), AXES, split_axi...]
    dot_general x16, matrix products: 9.47 us -> 5.88 us  [mm(): return jnp.einsum('mij,mjk->mik', a, b, precision=HI)]
    all_to_all x2 -> x0, local copies, waits for them, and re-layouts: 2.97 us -> none  [the longest x1 1.77 us: on_device(): lax.all_to_all(new_momentum, 'shard', split_axis=0, concat_axis=1, tiled=...]
  transfers between devices with their start and end apart: 7 -> 22, of which waited for: 7 -> 10; matrix products, arithmetic and copies ran while one was open for 0% -> 9% of each run, Pallas kernels for 0% -> 0%
where the time goes in v3:
time: 137 us; the launch traced here: 134 us
  waiting for transfers between devices  55.4 us (40%)
  starting transfers between devices  43.2 us (32%)
  Pallas kernels  11.1 us (8%)
  other arithmetic  10.5 us (8%)
  matrix products  8.08 us (6%)
  local copies, waits for them, and re-layouts  4.68 us (3%)
    ppermute x20, waiting for transfers between devices, swap(): return lax.ppermute(x, axis, [(i, i ^ bits) for i in range(size)])  41.2 us
    ppermute x20, starting transfers between devices, swap(): return lax.ppermute(x, axis, [(i, i ^ bits) for i in range(size)])  30.6 us
    all_to_all x1, waiting for transfers between devices, mixed(): first = lax.all_to_all(first, AXES, split_axis=0, concat_axis=0, tiled=True)  14.2 us
    pallas_call x1, Pallas kernels, whole(): pl.pallas_call(functools.partial(whole_kernel, shards, model, rows, cols)...  11.1 us
    all_to_all x1, starting transfers between devices, mixed(): lax.all_to_all(first.reshape(shards * model, rows, cols), AXES, split_axi...  8.11 us
    dot_general x16, matrix products, mm(): return jnp.einsum('mij,mjk->mik', a, b, precision=HI)  5.88 us
    all_to_all x1, starting transfers between devices, mixed(): first = lax.all_to_all(first, AXES, split_axis=0, concat_axis=0, tiled=True)  4.53 us
    add x1, other arithmetic, mixed(): new_momentum = hold_rate * moment_stack + grad_stack  3.4 us
  transfers between devices with their start and end apart: 22, of which 10 were waited for; matrix products, arithmetic and copies ran while one was open for 9% of the time, Pallas kernels for 0%

profile of v3, /device:TPU:0, one launch (start us, length us, event | category | flops | bytes accessed | tf_op | source)
XLA Modules:
  0.0 134.1 jit_solution(1935403936444979496)
XLA Ops:
  0.7 3.0 %slice_add_fusion = f32[8,4,16,512]{3,2,1,0:T(8,128)} fusion(f32[8,8,16,512]{3,2,1,0:T(8,128)} %bitcast.140, f32[8,8,16,512]{3,2,1,0:T(8,128)} %bitcast.141), kind=kLoop, calls=%fused_computation.10 | loop fusion | flops 524288 | bytes 3145728 | tf_op jit(solution)/shard_map/add | solution.py:163
  3.6 3.4 %multiply_add_fusion = f32[64,16,512]{2,1,0:T(8,128)} fusion(f32[64,16,512]{2,1,0:T(8,128)S(1)} %copy-done.1, f32[64,16,512]{2,1,0:T(8,128)} %param.6), kind=kLoop, calls=%fused_computation | loop fusion | flops 1048576 | bytes 6291456 | tf_op jit(solution)/shard_map/add | solution.py:165
  7.0 1.3 dynamic-slice_bitcast_fusion
  8.3 3.0 %collective-permute-start = (f32[4,16,512]{2,1,0:T(8,128)S(1)}, f32[4,16,512]{2,1,0:T(8,128)S(1)}, u32[]{:S(2)}, u32[]{:S(2)}) collective-permute-start(f32[4,16,512]{2,1,0:T(8,128)S(1)} %get-tuple-element.26), channel_id=1, source_target_pairs={{0,4},{4,0},{8,12},{12,8},{16,20},{20,16},{24,28},{28,24},{1,5},{5... | collective-permute-start | bytes 393224 | tf_op jit(solution)/shard_map/ppermute | solution.py:123
  11.4 1.6 %collective-permute-start.1 = (f32[4,16,512]{2,1,0:T(8,128)S(1)}, f32[4,16,512]{2,1,0:T(8,128)S(1)}, u32[]{:S(2)}, u32[]{:S(2)}) collective-permute-start(f32[4,16,512]{2,1,0:T(8,128)S(1)} %get-tuple-element.25), channel_id=1, source_target_pairs={{0,8},{4,12},{8,0},{12,4},{16,24},{20,28},{24,16},{28,20},{1,9},{5... | collective-permute-start | bytes 393224 | tf_op jit(solution)/shard_map/ppermute | solution.py:123
  13.0 3.0 %collective-permute-start.3 = (f32[4,16,512]{2,1,0:T(8,128)S(1)}, f32[4,16,512]{2,1,0:T(8,128)S(1)}, u32[]{:S(2)}, u32[]{:S(2)}) collective-permute-start(f32[4,16,512]{2,1,0:T(8,128)S(1)} %get-tuple-element.23), channel_id=1, source_target_pairs={{0,16},{4,20},{8,24},{12,28},{16,0},{20,4},{24,8},{28,12},{1,17},{... | collective-permute-start | bytes 393224 | tf_op jit(solution)/shard_map/ppermute | solution.py:123
  16.0 1.3 collective-permute-start.4
  17.2 0.9 bitcast_dynamic-update-slice_fusion
  18.2 3.7 %collective-permute-start.5 = (f32[4,16,512]{2,1,0:T(8,128)S(1)}, f32[4,16,512]{2,1,0:T(8,128)S(1)}, u32[]{:S(2)}, u32[]{:S(2)}) collective-permute-start(f32[4,16,512]{2,1,0:T(8,128)S(1)} %get-tuple-element.21), channel_id=1, source_target_pairs={{0,24},{4,28},{8,16},{12,20},{16,8},{20,12},{24,0},{28,4},{1,25},{... | collective-permute-start | bytes 393224 | tf_op jit(solution)/shard_map/ppermute | solution.py:123
  21.8 0.3 collective-permute-done.1
  22.1 0.8 collective-permute-start.6
  23.0 12.4 %collective-permute-done.4 = f32[4,16,512]{2,1,0:T(8,128)S(1)} collective-permute-done((f32[4,16,512]{2,1,0:T(8,128)S(1)}, f32[4,16,512]{2,1,0:T(8,128)S(1)}, u32[]{:S(2)}, u32[]{:S(2)}) %collective-permute-start.4) | collective-permute-done | bytes 131104 | tf_op jit(solution)/shard_map/ppermute | solution.py:123
  35.4 1.1 fusion.38
  36.6 0.1 collective-permute-start.7
  36.6 8.1 %all-to-all-start = ((f32[32,16,512]{2,1,0:T(8,128)}), f32[32,16,512]{2,1,0:T(8,128)}, u32[]{:S(2)}, u32[]{:S(2)}) async-start(f32[32,16,512]{2,1,0:T(8,128)} %bitcast.3), calls=%async_computation | async-start | bytes 2097152 | tf_op jit(solution)/shard_map/all_to_all | solution.py:167
  44.8 1.8 %collective-permute-start.8 = (f32[2,128,128]{2,1,0:T(8,128)S(1)}, f32[2,128,128]{2,1,0:T(8,128)S(1)}, u32[]{:S(2)}, u32[]{:S(2)}) collective-permute-start(f32[2,128,128]{2,1,0:T(8,128)S(1)} %dynamic-slice_add_fusion.1), channel_id=1, source_target_pairs={{0,2},{1,3},{2,0},{3,1},{4,6},{5,7},{6,4},{7,5},{8,10},{9,11},{10,... | collective-permute-start | bytes 393224 | tf_op jit(solution)/shard_map/ppermute | solution.py:123
  46.6 11.1 %collective-permute-done.8 = f32[2,128,128]{2,1,0:T(8,128)S(1)} collective-permute-done((f32[2,128,128]{2,1,0:T(8,128)S(1)}, f32[2,128,128]{2,1,0:T(8,128)S(1)}, u32[]{:S(2)}, u32[]{:S(2)}) %collective-permute-start.8) | collective-permute-done | bytes 131104 | tf_op jit(solution)/shard_map/ppermute | solution.py:123
  57.7 0.1 select_reduce_fusion
  57.8 0.3 add_add_fusion.1
  58.2 0.3 fusion.27
  58.5 0.3 fusion.39
  58.8 0.3 fusion.2
  59.1 0.3 convolution_multiply_fusion.3
  59.4 0.1 collective-permute-start.9
  59.4 1.3 collective-permute-done.9
  60.8 1.0 fusion.4
  61.8 1.1 fusion.40
  62.9 0.2 collective-permute-start.10
  63.1 1.2 collective-permute-done.10
  64.3 1.1 collective-permute-start.11
  65.4 6.3 %collective-permute-done.11 = f32[2,128,128]{2,1,0:T(8,128)S(1)} collective-permute-done((f32[2,128,128]{2,1,0:T(8,128)S(1)}, f32[2,128,128]{2,1,0:T(8,128)S(1)}, u32[]{:S(2)}, u32[]{:S(2)}) %collective-permute-start.11) | collective-permute-done | bytes 131104 | tf_op jit(solution)/shard_map/ppermute | solution.py:123
  71.7 0.3 add_add_fusion
  72.0 0.3 fusion.41
  72.2 0.3 fusion.42
  72.5 11.1 %shard_map.50 = f32[32,16,512]{2,1,0:T(8,128)} custom-call(f32[32,16,512]{2,1,0:T(8,128)} %all-to-all-done.x_ref), custom_call_target="tpu_custom_call" | custom-call | flops 1610612736 | bytes 2097152 | tf_op jit(solution)/shard_map/pallas_call | solution.py:94
  83.6 4.5 %all-to-all-start.1 = ((f32[32,16,512]{2,1,0:T(8,128)}), f32[32,16,512]{2,1,0:T(8,128)}, u32[]{:S(2)}, u32[]{:S(2)}) async-start(f32[32,16,512]{2,1,0:T(8,128)} %shard_map.50), calls=%async_computation.1 | async-start | bytes 2097152 | tf_op jit(solution)/shard_map/all_to_all | solution.py:172
  88.2 0.0 copy-start.3
  88.2 0.3 fusion.1
  88.4 0.3 fusion.43
  88.7 0.3 fusion.45
  89.0 0.3 fusion.44
  89.3 0.3 fusion
  89.5 0.3 fusion.46
  89.8 0.1 collective-permute-start.12
  89.9 0.2 broadcast_multiply_fusion
  90.2 1.1 collective-permute-done.12
  91.2 1.0 fusion.10
  92.3 0.9 copy-done.2
  93.2 0.1 slice_bitcast_fusion
  93.3 1.6 %collective-permute-start.13 = (f32[4,16,512]{2,1,0:T(8,128)S(1)}, f32[4,16,512]{2,1,0:T(8,128)}, u32[]{:S(2)}, u32[]{:S(2)}) collective-permute-start(f32[4,16,512]{2,1,0:T(8,128)S(1)} %get-tuple-element.33), channel_id=1, source_target_pairs={{0,4},{4,0},{8,12},{12,8},{16,20},{20,16},{24,28},{28,24},{1,5},{5... | collective-permute-start | bytes 393224 | tf_op jit(solution)/shard_map/ppermute | solution.py:123
  94.9 1.5 %collective-permute-start.14 = (f32[4,16,512]{2,1,0:T(8,128)S(1)}, f32[4,16,512]{2,1,0:T(8,128)S(1)}, u32[]{:S(2)}, u32[]{:S(2)}) collective-permute-start(f32[4,16,512]{2,1,0:T(8,128)S(1)} %get-tuple-element.32), channel_id=1, source_target_pairs={{0,8},{4,12},{8,0},{12,4},{16,24},{20,28},{24,16},{28,20},{1,9},{5... | collective-permute-start | bytes 393224 | tf_op jit(solution)/shard_map/ppermute | solution.py:123
  96.3 0.5 collective-permute-start.15
  96.8 2.4 %collective-permute-start.16 = (f32[4,16,512]{2,1,0:T(8,128)S(1)}, f32[4,16,512]{2,1,0:T(8,128)S(1)}, u32[]{:S(2)}, u32[]{:S(2)}) collective-permute-start(f32[4,16,512]{2,1,0:T(8,128)S(1)} %get-tuple-element.30), channel_id=1, source_target_pairs={{0,16},{4,20},{8,24},{12,28},{16,0},{20,4},{24,8},{28,12},{1,17},{... | collective-permute-start | bytes 393224 | tf_op jit(solution)/shard_map/ppermute | solution.py:123
  99.3 1.5 %collective-permute-start.17 = (f32[4,16,512]{2,1,0:T(8,128)S(1)}, f32[4,16,512]{2,1,0:T(8,128)S(1)}, u32[]{:S(2)}, u32[]{:S(2)}) collective-permute-start(f32[4,16,512]{2,1,0:T(8,128)S(1)} %get-tuple-element.29), channel_id=1, source_target_pairs={{0,20},{4,16},{8,28},{12,24},{16,4},{20,0},{24,12},{28,8},{1,21},{... | collective-permute-start | bytes 393224 | tf_op jit(solution)/shard_map/ppermute | solution.py:123
  100.7 14.2 %all-to-all-done.1 = f32[32,16,512]{2,1,0:T(8,128)} async-done(((f32[32,16,512]{2,1,0:T(8,128)}), f32[32,16,512]{2,1,0:T(8,128)}, u32[]{:S(2)}, u32[]{:S(2)}) %all-to-all-start.1) | async-done | bytes 1048608 | tf_op jit(solution)/shard_map/all_to_all | solution.py:172
  114.9 1.3 broadcast_multiply_fusion.1
  116.3 0.3 fusion.3
  116.5 0.9 fusion.17
  117.5 6.5 %collective-permute-start.18 = (f32[4,16,512]{2,1,0:T(8,128)S(1)}, f32[4,16,512]{2,1,0:T(8,128)S(1)}, u32[]{:S(2)}, u32[]{:S(2)}) collective-permute-start(f32[4,16,512]{2,1,0:T(8,128)S(1)} %get-tuple-element.28), channel_id=1, source_target_pairs={{0,24},{4,28},{8,16},{12,20},{16,8},{20,12},{24,0},{28,4},{1,25},{... | collective-permute-start | bytes 393224 | tf_op jit(solution)/shard_map/ppermute | solution.py:123
  124.0 0.9 fusion.24
  125.0 0.1 collective-permute-start.19
  125.2 5.8 %collective-permute-done.17 = f32[4,16,512]{2,1,0:T(8,128)S(1)} collective-permute-done((f32[4,16,512]{2,1,0:T(8,128)S(1)}, f32[4,16,512]{2,1,0:T(8,128)S(1)}, u32[]{:S(2)}, u32[]{:S(2)}) %collective-permute-start.17) | collective-permute-done | bytes 131104 | tf_op jit(solution)/shard_map/ppermute | solution.py:123
  131.1 1.7 %collective-permute-done.19 = f32[4,16,512]{2,1,0:T(8,128)S(1)} collective-permute-done((f32[4,16,512]{2,1,0:T(8,128)S(1)}, f32[4,16,512]{2,1,0:T(8,128)S(1)}, u32[]{:S(2)}, u32[]{:S(2)}) %collective-permute-start.19) | collective-permute-done | bytes 131104 | tf_op jit(solution)/shard_map/ppermute | solution.py:123
  132.8 1.3 copy-done
  (39 shorter events, 0.4 us)
Async XLA Ops:
  0.6 3.0 %copy-start.1 = (f32[64,16,512]{2,1,0:T(8,128)S(1)}, f32[64,16,512]{2,1,0:T(8,128)}, u32[]{:S(2)}) copy-start(f32[64,16,512]{2,1,0:T(8,128)} %param.5) | copy-start | bytes 6291460
  8.3 9.8 %collective-permute-start = (f32[4,16,512]{2,1,0:T(8,128)S(1)}, f32[4,16,512]{2,1,0:T(8,128)S(1)}, u32[]{:S(2)}, u32[]{:S(2)}) collective-permute-start(f32[4,16,512]{2,1,0:T(8,128)S(1)} %get-tuple-element.26), channel_id=1, source_target_pairs={{0,4},{4,0},{8,12},{12,8},{16,20},{20,16},{24,28},{28,24},{1,5},{5... | collective-permute-start | bytes 393224 | tf_op jit(solution)/shard_map/ppermute | solution.py:123
  11.4 10.8 %collective-permute-start.1 = (f32[4,16,512]{2,1,0:T(8,128)S(1)}, f32[4,16,512]{2,1,0:T(8,128)S(1)}, u32[]{:S(2)}, u32[]{:S(2)}) collective-permute-start(f32[4,16,512]{2,1,0:T(8,128)S(1)} %get-tuple-element.25), channel_id=1, source_target_pairs={{0,8},{4,12},{8,0},{12,4},{16,24},{20,28},{24,16},{28,20},{1,9},{5... | collective-permute-start | bytes 393224 | tf_op jit(solution)/shard_map/ppermute | solution.py:123
  13.0 10.0 %collective-permute-start.2 = (f32[4,16,512]{2,1,0:T(8,128)S(1)}, f32[4,16,512]{2,1,0:T(8,128)S(1)}, u32[]{:S(2)}, u32[]{:S(2)}) collective-permute-start(f32[4,16,512]{2,1,0:T(8,128)S(1)} %get-tuple-element.24), channel_id=1, source_target_pairs={{0,12},{4,8},{8,4},{12,0},{16,28},{20,24},{24,20},{28,16},{1,13},{... | collective-permute-start | bytes 393224 | tf_op jit(solution)/shard_map/ppermute | solution.py:123
  13.0 10.0 %collective-permute-start.3 = (f32[4,16,512]{2,1,0:T(8,128)S(1)}, f32[4,16,512]{2,1,0:T(8,128)S(1)}, u32[]{:S(2)}, u32[]{:S(2)}) collective-permute-start(f32[4,16,512]{2,1,0:T(8,128)S(1)} %get-tuple-element.23), channel_id=1, source_target_pairs={{0,16},{4,20},{8,24},{12,28},{16,0},{20,4},{24,8},{28,12},{1,17},{... | collective-permute-start | bytes 393224 | tf_op jit(solution)/shard_map/ppermute | solution.py:123
  16.0 19.4 %collective-permute-start.4 = (f32[4,16,512]{2,1,0:T(8,128)S(1)}, f32[4,16,512]{2,1,0:T(8,128)S(1)}, u32[]{:S(2)}, u32[]{:S(2)}) collective-permute-start(f32[4,16,512]{2,1,0:T(8,128)S(1)} %get-tuple-element.22), channel_id=1, source_target_pairs={{0,20},{4,16},{8,28},{12,24},{16,4},{20,0},{24,12},{28,8},{1,21},{... | collective-permute-start | bytes 393224 | tf_op jit(solution)/shard_map/ppermute | solution.py:123
  18.2 17.2 %collective-permute-start.5 = (f32[4,16,512]{2,1,0:T(8,128)S(1)}, f32[4,16,512]{2,1,0:T(8,128)S(1)}, u32[]{:S(2)}, u32[]{:S(2)}) collective-permute-start(f32[4,16,512]{2,1,0:T(8,128)S(1)} %get-tuple-element.21), channel_id=1, source_target_pairs={{0,24},{4,28},{8,16},{12,20},{16,8},{20,12},{24,0},{28,4},{1,25},{... | collective-permute-start | bytes 393224 | tf_op jit(solution)/shard_map/ppermute | solution.py:123
  22.1 13.3 %collective-permute-start.6 = (f32[4,16,512]{2,1,0:T(8,128)S(1)}, f32[4,16,512]{2,1,0:T(8,128)S(1)}, u32[]{:S(2)}, u32[]{:S(2)}) collective-permute-start(f32[4,16,512]{2,1,0:T(8,128)S(1)} %get-tuple-element.20), channel_id=1, source_target_pairs={{0,28},{4,24},{8,20},{12,16},{16,12},{20,8},{24,4},{28,0},{1,29},{... | collective-permute-start | bytes 393224 | tf_op jit(solution)/shard_map/ppermute | solution.py:123
  36.6 8.2 %collective-permute-start.7 = (f32[2,128,128]{2,1,0:T(8,128)S(1)}, f32[2,128,128]{2,1,0:T(8,128)S(1)}, u32[]{:S(2)}, u32[]{:S(2)}) collective-permute-start(f32[2,128,128]{2,1,0:T(8,128)S(1)} %constant_dynamic-slice_fusion.1), channel_id=1, source_target_pairs={{0,1},{1,0},{2,3},{3,2},{4,5},{5,4},{6,7},{7,6},{8,9},{9,8},{10,11... | collective-permute-start | bytes 393224 | tf_op jit(solution)/shard_map/ppermute | solution.py:123
  36.6 35.9 %all-to-all-start = ((f32[32,16,512]{2,1,0:T(8,128)}), f32[32,16,512]{2,1,0:T(8,128)}, u32[]{:S(2)}, u32[]{:S(2)}) async-start(f32[32,16,512]{2,1,0:T(8,128)} %bitcast.3), calls=%async_computation | async-start | bytes 2097152 | tf_op jit(solution)/shard_map/all_to_all | solution.py:167
  44.8 12.9 %collective-permute-start.8 = (f32[2,128,128]{2,1,0:T(8,128)S(1)}, f32[2,128,128]{2,1,0:T(8,128)S(1)}, u32[]{:S(2)}, u32[]{:S(2)}) collective-permute-start(f32[2,128,128]{2,1,0:T(8,128)S(1)} %dynamic-slice_add_fusion.1), channel_id=1, source_target_pairs={{0,2},{1,3},{2,0},{3,1},{4,6},{5,7},{6,4},{7,5},{8,10},{9,11},{10,... | collective-permute-start | bytes 393224 | tf_op jit(solution)/shard_map/ppermute | solution.py:123
  59.4 1.4 %collective-permute-start.9 = (f32[2,128,128]{2,1,0:T(8,128)S(1)}, f32[2,128,128]{2,1,0:T(8,128)S(1)}, u32[]{:S(2)}, u32[]{:S(2)}) collective-permute-start(f32[2,128,128]{2,1,0:T(8,128)S(1)} %convolution_multiply_fusion.3), channel_id=1, source_target_pairs={{0,1},{1,0},{2,3},{3,2},{4,5},{5,4},{6,7},{7,6},{8,9},{9,8},{10,11... | collective-permute-start | bytes 393224 | tf_op jit(solution)/shard_map/ppermute | solution.py:123
  62.9 1.4 %collective-permute-start.10 = (f32[2,128,128]{2,1,0:T(8,128)S(1)}, f32[2,128,128]{2,1,0:T(8,128)S(1)}, u32[]{:S(2)}, u32[]{:S(2)}) collective-permute-start(f32[2,128,128]{2,1,0:T(8,128)S(1)} %constant_dynamic-slice_fusion), channel_id=1, source_target_pairs={{0,1},{1,0},{2,3},{3,2},{4,5},{5,4},{6,7},{7,6},{8,9},{9,8},{10,11... | collective-permute-start | bytes 393224 | tf_op jit(solution)/shard_map/ppermute | solution.py:123
  64.3 7.3 %collective-permute-start.11 = (f32[2,128,128]{2,1,0:T(8,128)S(1)}, f32[2,128,128]{2,1,0:T(8,128)S(1)}, u32[]{:S(2)}, u32[]{:S(2)}) collective-permute-start(f32[2,128,128]{2,1,0:T(8,128)S(1)} %dynamic-slice_add_fusion), channel_id=1, source_target_pairs={{0,2},{1,3},{2,0},{3,1},{4,6},{5,7},{6,4},{7,5},{8,10},{9,11},{10,... | collective-permute-start | bytes 393224 | tf_op jit(solution)/shard_map/ppermute | solution.py:123
  83.6 31.3 %all-to-all-start.1 = ((f32[32,16,512]{2,1,0:T(8,128)}), f32[32,16,512]{2,1,0:T(8,128)}, u32[]{:S(2)}, u32[]{:S(2)}) async-start(f32[32,16,512]{2,1,0:T(8,128)} %shard_map.50), calls=%async_computation.1 | async-start | bytes 2097152 | tf_op jit(solution)/shard_map/all_to_all | solution.py:172
  88.2 1.7 %copy-start.3 = (f32[64,16,512]{2,1,0:T(8,128)S(1)}, f32[64,16,512]{2,1,0:T(8,128)}, u32[]{:S(2)}) copy-start(f32[64,16,512]{2,1,0:T(8,128)} %param.7) | copy-start | bytes 6291460
  89.8 1.4 %collective-permute-start.12 = (f32[2,128,128]{2,1,0:T(8,128)S(1)}, f32[2,128,128]{2,1,0:T(8,128)S(1)}, u32[]{:S(2)}, u32[]{:S(2)}) collective-permute-start(f32[2,128,128]{2,1,0:T(8,128)S(1)} %fusion.46), channel_id=1, source_target_pairs={{0,1},{1,0},{2,3},{3,2},{4,5},{5,4},{6,7},{7,6},{8,9},{9,8},{10,11... | collective-permute-start | bytes 393224 | tf_op jit(solution)/shard_map/ppermute | solution.py:123
  92.2 1.0 copy-start.2
  93.3 24.2 %collective-permute-start.13 = (f32[4,16,512]{2,1,0:T(8,128)S(1)}, f32[4,16,512]{2,1,0:T(8,128)}, u32[]{:S(2)}, u32[]{:S(2)}) collective-permute-start(f32[4,16,512]{2,1,0:T(8,128)S(1)} %get-tuple-element.33), channel_id=1, source_target_pairs={{0,4},{4,0},{8,12},{12,8},{16,20},{20,16},{24,28},{28,24},{1,5},{5... | collective-permute-start | bytes 393224 | tf_op jit(solution)/shard_map/ppermute | solution.py:123
  94.9 30.1 %collective-permute-start.14 = (f32[4,16,512]{2,1,0:T(8,128)S(1)}, f32[4,16,512]{2,1,0:T(8,128)S(1)}, u32[]{:S(2)}, u32[]{:S(2)}) collective-permute-start(f32[4,16,512]{2,1,0:T(8,128)S(1)} %get-tuple-element.32), channel_id=1, source_target_pairs={{0,8},{4,12},{8,0},{12,4},{16,24},{20,28},{24,16},{28,20},{1,9},{5... | collective-permute-start | bytes 393224 | tf_op jit(solution)/shard_map/ppermute | solution.py:123
  96.3 28.7 %collective-permute-start.15 = (f32[4,16,512]{2,1,0:T(8,128)S(1)}, f32[4,16,512]{2,1,0:T(8,128)S(1)}, u32[]{:S(2)}, u32[]{:S(2)}) collective-permute-start(f32[4,16,512]{2,1,0:T(8,128)S(1)} %get-tuple-element.31), channel_id=1, source_target_pairs={{0,12},{4,8},{8,4},{12,0},{16,28},{20,24},{24,20},{28,16},{1,13},{... | collective-permute-start | bytes 393224 | tf_op jit(solution)/shard_map/ppermute | solution.py:123
  96.8 28.3 %collective-permute-start.16 = (f32[4,16,512]{2,1,0:T(8,128)S(1)}, f32[4,16,512]{2,1,0:T(8,128)S(1)}, u32[]{:S(2)}, u32[]{:S(2)}) collective-permute-start(f32[4,16,512]{2,1,0:T(8,128)S(1)} %get-tuple-element.30), channel_id=1, source_target_pairs={{0,16},{4,20},{8,24},{12,28},{16,0},{20,4},{24,8},{28,12},{1,17},{... | collective-permute-start | bytes 393224 | tf_op jit(solution)/shard_map/ppermute | solution.py:123
  99.3 31.7 %collective-permute-start.17 = (f32[4,16,512]{2,1,0:T(8,128)S(1)}, f32[4,16,512]{2,1,0:T(8,128)S(1)}, u32[]{:S(2)}, u32[]{:S(2)}) collective-permute-start(f32[4,16,512]{2,1,0:T(8,128)S(1)} %get-tuple-element.29), channel_id=1, source_target_pairs={{0,20},{4,16},{8,28},{12,24},{16,4},{20,0},{24,12},{28,8},{1,21},{... | collective-permute-start | bytes 393224 | tf_op jit(solution)/shard_map/ppermute | solution.py:123
  117.5 13.5 %collective-permute-start.18 = (f32[4,16,512]{2,1,0:T(8,128)S(1)}, f32[4,16,512]{2,1,0:T(8,128)S(1)}, u32[]{:S(2)}, u32[]{:S(2)}) collective-permute-start(f32[4,16,512]{2,1,0:T(8,128)S(1)} %get-tuple-element.28), channel_id=1, source_target_pairs={{0,24},{4,28},{8,16},{12,20},{16,8},{20,12},{24,0},{28,4},{1,25},{... | collective-permute-start | bytes 393224 | tf_op jit(solution)/shard_map/ppermute | solution.py:123
  125.0 7.8 %collective-permute-start.19 = (f32[4,16,512]{2,1,0:T(8,128)S(1)}, f32[4,16,512]{2,1,0:T(8,128)S(1)}, u32[]{:S(2)}, u32[]{:S(2)}) collective-permute-start(f32[4,16,512]{2,1,0:T(8,128)S(1)} %get-tuple-element.27), channel_id=1, source_target_pairs={{0,28},{4,24},{8,20},{12,16},{16,12},{20,8},{24,4},{28,0},{1,29},{... | collective-permute-start | bytes 393224 | tf_op jit(solution)/shard_map/ppermute | solution.py:123
  132.8 1.3 copy-start

commit v4 on v3

--- a/solution.py
+++ b/solution.py
@@ -22,10 +22,6 @@
 
 def dot(a, b):
     return lax.dot_general(a, b, (((1,), (0,)), ((), ())), precision=HI, preferred_element_type=F32)
-
-
-def dot_t(a, b):
-    return lax.dot_general(a, b, (((1,), (1,)), ((), ())), precision=HI, preferred_element_type=F32)
 
 
 def eye_of(n):
@@ -51,41 +47,73 @@
     return lax.rsqrt(jnp.sum(gram * eye, axis=(0, 1), keepdims=True) + 1e-06)
 
 
+def parts3(x):
+    h = x.astype(jnp.bfloat16)
+    rest = x - h.astype(F32)
+    m = rest.astype(jnp.bfloat16)
+    return h, m, (rest - m.astype(F32)).astype(jnp.bfloat16)
+
+
+def bdot(a, b):
+    return lax.dot_general(a, b, (((1,), (0,)), ((), ())), preferred_element_type=F32)
+
+
+def bdot_t(a, b):
+    return lax.dot_general(a, b, (((1,), (1,)), ((), ())), preferred_element_type=F32)
+
+
+def left_of(q):
+    h, m, l = parts3(q)
+    return jnp.concatenate([h, m], axis=1), jnp.concatenate([l, h], axis=1), jnp.concatenate([m, h], axis=1)
+
+
+def times(left, x):
+    h, m, l = x
+    first, second, third = left
+    return (bdot(second, jnp.concatenate([h, l], axis=0)) + bdot(third, jnp.concatenate([m, m], axis=0))) + bdot(
+        first, jnp.concatenate([h, h], axis=0))
+
+
+def gram_parts(x):
+    h, m, l = x
+    return bdot_t(h, h) + bdot_t(m, m), bdot_t(jnp.concatenate([h, h], axis=1), jnp.concatenate([m, l], axis=1))
+
+
 def whole_kernel(shards, model, rows, cols, x_ref, o_ref, a_ref):
-    eye = eye_of(shards * rows)
-
-    def load(s, _):
-        for m in range(model):
-            a_ref[pl.ds(pl.multiple_of(s * rows, rows), rows), m * cols:(m + 1) * cols] = x_ref[s * model + m]
-        return 0
-
-    lax.fori_loop(0, shards, load, 0)
-
-    def gram(m, total):
-        at = pl.ds(pl.multiple_of(m * cols, cols), cols)
-        return total + dot_t(a_ref[:, at], a_ref[:, at])
-
+    side = shards * rows
+    eye = eye_of(side)
     zero = jnp.zeros(eye.shape, F32)
-    g = lax.fori_loop(0, model, gram, zero)
+
+    def add(totals, x):
+        return tuple(t + p for t, p in zip(totals, gram_parts(x)))
+
+    def store(at, x):
+        for k in range(3):
+            a_ref[k, :, at] = x[k]
+
+    totals = (zero, zero)
+    for m in range(model):
+        x = parts3(jnp.concatenate([x_ref[s * model + m] for s in range(shards)], axis=0))
+        store(slice(m * cols, (m + 1) * cols), x)
+        totals = add(totals, x)
+    g = totals[0] + (totals[1] + totals[1].T)
     norm = inverse_norm(g, eye)
-    q = chain([g * (norm * norm)], EARLY, eye)[0] * norm
-
-    def early(m, total):
-        at = pl.ds(pl.multiple_of(m * cols, cols), cols)
-        y = dot(q, a_ref[:, at])
-        a_ref[:, at] = y
-        return total + dot_t(y, y)
-
-    g = lax.fori_loop(0, model, early, zero)
-    r = chain([g], ITERS - EARLY, eye)[0]
-
-    def late(m, _):
-        y = dot(r, a_ref[:, pl.ds(pl.multiple_of(m * cols, cols), cols)])
+    left = left_of(chain([g * (norm * norm)], EARLY, eye)[0] * norm)
+
+    totals = (zero, zero)
+    for m in range(model):
+        at = slice(m * cols, (m + 1) * cols)
+        x = parts3(times(left, tuple(a_ref[k, :, at] for k in range(3))))
+        store(at, x)
+        totals = add(totals, x)
+    g = totals[0] + (totals[1] + totals[1].T)
+    left = left_of(chain([g], ITERS - EARLY, eye)[0])
+
+    for m in range(model):
+        at = slice(m * cols, (m + 1) * cols)
+        y = times(left, tuple(a_ref[k, :, at] for k in range(3)))
         for s in range(shards):
             o_ref[s * model + m] = y[s * rows:(s + 1) * rows]
-        return 0
-
-    lax.fori_loop(0, model, late, 0)
 
 
 def whole(x, shards, model):
@@ -96,7 +124,7 @@
         out_shape=jax.ShapeDtypeStruct(x.shape, F32),
         in_specs=[VMEM],
         out_specs=VMEM,
-        scratch_shapes=[pltpu.VMEM((shards * rows, model * cols), F32)],
+        scratch_shapes=[pltpu.VMEM((3, shards * rows, model * cols), jnp.bfloat16)],
         cost_estimate=pl.CostEstimate(flops=flops, bytes_accessed=8 * x.size, transcendentals=0),
     )(x)
 
@@ -139,7 +167,7 @@
 
 
 def spread(x, model):
-    eye = jnp.eye(x.shape[1], dtype=F32)
+    eye = lax.optimization_barrier(jnp.eye(x.shape[1], dtype=F32))
     g = gram_of(x)
     g = summed(g, model)
     r = lax.rsqrt(jnp.einsum("mii->m", g) + 1e-06)[:, None, None]
@@ -176,7 +204,7 @@
     second = [x[:, d] for d in range(shards)]
     second = direct(second, shards)
 
-    kept = lax.optimization_barrier((1.0 - learn_rate * decay_rate) * weight_stack.reshape(cut))
+    kept = (1.0 - learn_rate * decay_rate) * weight_stack.reshape(cut)
     total = kept.at[:, :w].add(-learn_rate * first.reshape(shards, w, rows, cols))
     for d in range(shards):
         at = (me ^ d, w, 0, 0)

time: 137 us -> 134 us (0.978)
  Pallas kernels: 11.1 us -> 8.17 us
    pallas_call x1, Pallas kernels: 11.1 us -> 8.17 us  [whole(): pl.pallas_call(functools.partial(whole_kernel, shards, model, rows, cols)...]
where the time goes in v4:
time: 134 us; the launch traced here: 131 us
  waiting for transfers between devices  55.4 us (41%)
  starting transfers between devices  43.2 us (32%)
  other arithmetic  10.5 us (8%)
  Pallas kernels  8.17 us (6%)
  matrix products  8.08 us (6%)
  local copies, waits for them, and re-layouts  4.68 us (3%)
    ppermute x20, waiting for transfers between devices, swap(): return lax.ppermute(x, axis, [(i, i ^ bits) for i in range(size)])  41.2 us
    ppermute x20, starting transfers between devices, swap(): return lax.ppermute(x, axis, [(i, i ^ bits) for i in range(size)])  30.6 us
    all_to_all x1, waiting for transfers between devices, mixed(): first = lax.all_to_all(first, AXES, split_axis=0, concat_axis=0, tiled=True)  14.2 us
    pallas_call x1, Pallas kernels, whole(): pl.pallas_call(functools.partial(whole_kernel, shards, model, rows, cols)...  8.17 us
    all_to_all x1, starting transfers between devices, mixed(): lax.all_to_all(first.reshape(shards * model, rows, cols), AXES, split_axi...  8.11 us
    dot_general x16, matrix products, mm(): return jnp.einsum('mij,mjk->mik', a, b, precision=HI)  5.88 us
    all_to_all x1, starting transfers between devices, mixed(): first = lax.all_to_all(first, AXES, split_axis=0, concat_axis=0, tiled=True)  4.53 us
    add x1, other arithmetic, mixed(): new_momentum = hold_rate * moment_stack + grad_stack  3.4 us
  transfers between devices with their start and end apart: 22, of which 10 were waited for; matrix products, arithmetic and copies ran while one was open for 9% of the time, Pallas kernels for 0%

profile of v4, /device:TPU:0, one launch (start us, length us, event | category | flops | bytes accessed | tf_op | source)
XLA Modules:
  0.0 131.2 jit_solution(1898332772030209454)
XLA Ops:
  0.7 3.0 %slice_add_fusion = f32[8,4,16,512]{3,2,1,0:T(8,128)} fusion(f32[8,8,16,512]{3,2,1,0:T(8,128)} %bitcast.140, f32[8,8,16,512]{3,2,1,0:T(8,128)} %bitcast.141), kind=kLoop, calls=%fused_computation.10 | loop fusion | flops 524288 | bytes 3145728 | tf_op jit(solution)/shard_map/add | solution.py:191
  3.6 3.4 %multiply_add_fusion = f32[64,16,512]{2,1,0:T(8,128)} fusion(f32[64,16,512]{2,1,0:T(8,128)S(1)} %copy-done.1, f32[64,16,512]{2,1,0:T(8,128)} %param.6), kind=kLoop, calls=%fused_computation | loop fusion | flops 1048576 | bytes 6291456 | tf_op jit(solution)/shard_map/add | solution.py:193
  7.0 1.3 dynamic-slice_bitcast_fusion
  8.3 3.0 %collective-permute-start = (f32[4,16,512]{2,1,0:T(8,128)S(1)}, f32[4,16,512]{2,1,0:T(8,128)S(1)}, u32[]{:S(2)}, u32[]{:S(2)}) collective-permute-start(f32[4,16,512]{2,1,0:T(8,128)S(1)} %get-tuple-element.26), channel_id=1, source_target_pairs={{0,4},{4,0},{8,12},{12,8},{16,20},{20,16},{24,28},{28,24},{1,5},{5... | collective-permute-start | bytes 393224 | tf_op jit(solution)/shard_map/ppermute | solution.py:151
  11.4 1.6 %collective-permute-start.1 = (f32[4,16,512]{2,1,0:T(8,128)S(1)}, f32[4,16,512]{2,1,0:T(8,128)S(1)}, u32[]{:S(2)}, u32[]{:S(2)}) collective-permute-start(f32[4,16,512]{2,1,0:T(8,128)S(1)} %get-tuple-element.25), channel_id=1, source_target_pairs={{0,8},{4,12},{8,0},{12,4},{16,24},{20,28},{24,16},{28,20},{1,9},{5... | collective-permute-start | bytes 393224 | tf_op jit(solution)/shard_map/ppermute | solution.py:151
  13.0 3.0 %collective-permute-start.3 = (f32[4,16,512]{2,1,0:T(8,128)S(1)}, f32[4,16,512]{2,1,0:T(8,128)S(1)}, u32[]{:S(2)}, u32[]{:S(2)}) collective-permute-start(f32[4,16,512]{2,1,0:T(8,128)S(1)} %get-tuple-element.23), channel_id=1, source_target_pairs={{0,16},{4,20},{8,24},{12,28},{16,0},{20,4},{24,8},{28,12},{1,17},{... | collective-permute-start | bytes 393224 | tf_op jit(solution)/shard_map/ppermute | solution.py:151
  16.0 1.3 collective-permute-start.4
  17.2 0.9 bitcast_dynamic-update-slice_fusion
  18.2 3.7 %collective-permute-start.5 = (f32[4,16,512]{2,1,0:T(8,128)S(1)}, f32[4,16,512]{2,1,0:T(8,128)S(1)}, u32[]{:S(2)}, u32[]{:S(2)}) collective-permute-start(f32[4,16,512]{2,1,0:T(8,128)S(1)} %get-tuple-element.21), channel_id=1, source_target_pairs={{0,24},{4,28},{8,16},{12,20},{16,8},{20,12},{24,0},{28,4},{1,25},{... | collective-permute-start | bytes 393224 | tf_op jit(solution)/shard_map/ppermute | solution.py:151
  21.8 0.3 collective-permute-done.1
  22.1 0.8 collective-permute-start.6
  23.0 12.4 %collective-permute-done.4 = f32[4,16,512]{2,1,0:T(8,128)S(1)} collective-permute-done((f32[4,16,512]{2,1,0:T(8,128)S(1)}, f32[4,16,512]{2,1,0:T(8,128)S(1)}, u32[]{:S(2)}, u32[]{:S(2)}) %collective-permute-start.4) | collective-permute-done | bytes 131104 | tf_op jit(solution)/shard_map/ppermute | solution.py:151
  35.4 1.1 fusion.38
  36.6 0.1 collective-permute-start.7
  36.6 8.1 %all-to-all-start = ((f32[32,16,512]{2,1,0:T(8,128)}), f32[32,16,512]{2,1,0:T(8,128)}, u32[]{:S(2)}, u32[]{:S(2)}) async-start(f32[32,16,512]{2,1,0:T(8,128)} %bitcast.3), calls=%async_computation | async-start | bytes 2097152 | tf_op jit(solution)/shard_map/all_to_all | solution.py:195
  44.8 1.8 %collective-permute-start.8 = (f32[2,128,128]{2,1,0:T(8,128)S(1)}, f32[2,128,128]{2,1,0:T(8,128)S(1)}, u32[]{:S(2)}, u32[]{:S(2)}) collective-permute-start(f32[2,128,128]{2,1,0:T(8,128)S(1)} %dynamic-slice_add_fusion.1), channel_id=1, source_target_pairs={{0,2},{1,3},{2,0},{3,1},{4,6},{5,7},{6,4},{7,5},{8,10},{9,11},{10,... | collective-permute-start | bytes 393224 | tf_op jit(solution)/shard_map/ppermute | solution.py:151
  46.6 11.1 %collective-permute-done.8 = f32[2,128,128]{2,1,0:T(8,128)S(1)} collective-permute-done((f32[2,128,128]{2,1,0:T(8,128)S(1)}, f32[2,128,128]{2,1,0:T(8,128)S(1)}, u32[]{:S(2)}, u32[]{:S(2)}) %collective-permute-start.8) | collective-permute-done | bytes 131104 | tf_op jit(solution)/shard_map/ppermute | solution.py:151
  57.7 0.1 select_reduce_fusion
  57.8 0.4 add_add_fusion.1
  58.2 0.3 fusion.27
  58.5 0.3 fusion.39
  58.8 0.3 fusion.2
  59.1 0.3 convolution_multiply_fusion.3
  59.4 0.1 collective-permute-start.9
  59.4 1.3 %collective-permute-done.9 = f32[2,128,128]{2,1,0:T(8,128)S(1)} collective-permute-done((f32[2,128,128]{2,1,0:T(8,128)S(1)}, f32[2,128,128]{2,1,0:T(8,128)S(1)}, u32[]{:S(2)}, u32[]{:S(2)}) %collective-permute-start.9) | collective-permute-done | bytes 131104 | tf_op jit(solution)/shard_map/ppermute | solution.py:151
  60.8 1.0 fusion.4
  61.8 1.1 fusion.40
  62.9 0.2 collective-permute-start.10
  63.1 1.2 collective-permute-done.10
  64.3 1.1 collective-permute-start.11
  65.4 6.3 %collective-permute-done.11 = f32[2,128,128]{2,1,0:T(8,128)S(1)} collective-permute-done((f32[2,128,128]{2,1,0:T(8,128)S(1)}, f32[2,128,128]{2,1,0:T(8,128)S(1)}, u32[]{:S(2)}, u32[]{:S(2)}) %collective-permute-start.11) | collective-permute-done | bytes 131104 | tf_op jit(solution)/shard_map/ppermute | solution.py:151
  71.7 0.3 add_add_fusion
  72.0 0.3 fusion.41
  72.2 0.3 fusion.42
  72.5 8.2 %shard_map.50 = f32[32,16,512]{2,1,0:T(8,128)} custom-call(f32[32,16,512]{2,1,0:T(8,128)} %all-to-all-done.x_ref), custom_call_target="tpu_custom_call" | custom-call | flops 1610612736 | bytes 2097152 | tf_op jit(solution)/shard_map/pallas_call | solution.py:122
  80.7 4.5 %all-to-all-start.1 = ((f32[32,16,512]{2,1,0:T(8,128)}), f32[32,16,512]{2,1,0:T(8,128)}, u32[]{:S(2)}, u32[]{:S(2)}) async-start(f32[32,16,512]{2,1,0:T(8,128)} %shard_map.50), calls=%async_computation.1 | async-start | bytes 2097152 | tf_op jit(solution)/shard_map/all_to_all | solution.py:200
  85.2 0.0 copy-start.3
  85.2 0.3 fusion.1
  85.5 0.3 fusion.43
  85.8 0.3 fusion.45
  86.1 0.3 fusion.44
  86.3 0.3 fusion
  86.6 0.3 fusion.46
  86.9 0.1 collective-permute-start.12
  87.0 0.2 broadcast_multiply_fusion
  87.2 1.1 collective-permute-done.12
  88.3 1.0 fusion.10
  89.3 0.9 copy-done.2
  90.3 0.1 slice_bitcast_fusion
  90.4 1.6 %collective-permute-start.13 = (f32[4,16,512]{2,1,0:T(8,128)S(1)}, f32[4,16,512]{2,1,0:T(8,128)}, u32[]{:S(2)}, u32[]{:S(2)}) collective-permute-start(f32[4,16,512]{2,1,0:T(8,128)S(1)} %get-tuple-element.33), channel_id=1, source_target_pairs={{0,4},{4,0},{8,12},{12,8},{16,20},{20,16},{24,28},{28,24},{1,5},{5... | collective-permute-start | bytes 393224 | tf_op jit(solution)/shard_map/ppermute | solution.py:151
  92.0 1.5 %collective-permute-start.14 = (f32[4,16,512]{2,1,0:T(8,128)S(1)}, f32[4,16,512]{2,1,0:T(8,128)S(1)}, u32[]{:S(2)}, u32[]{:S(2)}) collective-permute-start(f32[4,16,512]{2,1,0:T(8,128)S(1)} %get-tuple-element.32), channel_id=1, source_target_pairs={{0,8},{4,12},{8,0},{12,4},{16,24},{20,28},{24,16},{28,20},{1,9},{5... | collective-permute-start | bytes 393224 | tf_op jit(solution)/shard_map/ppermute | solution.py:151
  93.4 0.5 collective-permute-start.15
  93.9 2.4 %collective-permute-start.16 = (f32[4,16,512]{2,1,0:T(8,128)S(1)}, f32[4,16,512]{2,1,0:T(8,128)S(1)}, u32[]{:S(2)}, u32[]{:S(2)}) collective-permute-start(f32[4,16,512]{2,1,0:T(8,128)S(1)} %get-tuple-element.30), channel_id=1, source_target_pairs={{0,16},{4,20},{8,24},{12,28},{16,0},{20,4},{24,8},{28,12},{1,17},{... | collective-permute-start | bytes 393224 | tf_op jit(solution)/shard_map/ppermute | solution.py:151
  96.3 1.5 %collective-permute-start.17 = (f32[4,16,512]{2,1,0:T(8,128)S(1)}, f32[4,16,512]{2,1,0:T(8,128)S(1)}, u32[]{:S(2)}, u32[]{:S(2)}) collective-permute-start(f32[4,16,512]{2,1,0:T(8,128)S(1)} %get-tuple-element.29), channel_id=1, source_target_pairs={{0,20},{4,16},{8,28},{12,24},{16,4},{20,0},{24,12},{28,8},{1,21},{... | collective-permute-start | bytes 393224 | tf_op jit(solution)/shard_map/ppermute | solution.py:151
  97.8 14.2 %all-to-all-done.1 = f32[32,16,512]{2,1,0:T(8,128)} async-done(((f32[32,16,512]{2,1,0:T(8,128)}), f32[32,16,512]{2,1,0:T(8,128)}, u32[]{:S(2)}, u32[]{:S(2)}) %all-to-all-start.1) | async-done | bytes 1048608 | tf_op jit(solution)/shard_map/all_to_all | solution.py:200
  112.0 1.3 %broadcast_multiply_fusion.1 = f32[32,16,512]{2,1,0:T(8,128)S(1)} fusion(f32[32,16,512]{2,1,0:T(8,128)} %all-to-all-done.1), kind=kLoop, calls=%fused_computation.15 | loop fusion | flops 262144 | bytes 2097152 | tf_op jit(solution)/shard_map/mul | solution.py:208
  113.3 0.3 fusion.3
  113.6 0.9 fusion.17
  114.6 6.5 %collective-permute-start.18 = (f32[4,16,512]{2,1,0:T(8,128)S(1)}, f32[4,16,512]{2,1,0:T(8,128)S(1)}, u32[]{:S(2)}, u32[]{:S(2)}) collective-permute-start(f32[4,16,512]{2,1,0:T(8,128)S(1)} %get-tuple-element.28), channel_id=1, source_target_pairs={{0,24},{4,28},{8,16},{12,20},{16,8},{20,12},{24,0},{28,4},{1,25},{... | collective-permute-start | bytes 393224 | tf_op jit(solution)/shard_map/ppermute | solution.py:151
  121.1 0.9 fusion.24
  122.0 0.1 collective-permute-start.19
  122.2 5.8 %collective-permute-done.17 = f32[4,16,512]{2,1,0:T(8,128)S(1)} collective-permute-done((f32[4,16,512]{2,1,0:T(8,128)S(1)}, f32[4,16,512]{2,1,0:T(8,128)S(1)}, u32[]{:S(2)}, u32[]{:S(2)}) %collective-permute-start.17) | collective-permute-done | bytes 131104 | tf_op jit(solution)/shard_map/ppermute | solution.py:151
  128.1 1.7 %collective-permute-done.19 = f32[4,16,512]{2,1,0:T(8,128)S(1)} collective-permute-done((f32[4,16,512]{2,1,0:T(8,128)S(1)}, f32[4,16,512]{2,1,0:T(8,128)S(1)}, u32[]{:S(2)}, u32[]{:S(2)}) %collective-permute-start.19) | collective-permute-done | bytes 131104 | tf_op jit(solution)/shard_map/ppermute | solution.py:151
  129.9 1.3 copy-done
  (40 shorter events, 0.4 us)
Async XLA Ops:
  0.6 3.0 %copy-start.1 = (f32[64,16,512]{2,1,0:T(8,128)S(1)}, f32[64,16,512]{2,1,0:T(8,128)}, u32[]{:S(2)}) copy-start(f32[64,16,512]{2,1,0:T(8,128)} %param.5) | copy-start | bytes 6291460
  8.3 9.8 %collective-permute-start = (f32[4,16,512]{2,1,0:T(8,128)S(1)}, f32[4,16,512]{2,1,0:T(8,128)S(1)}, u32[]{:S(2)}, u32[]{:S(2)}) collective-permute-start(f32[4,16,512]{2,1,0:T(8,128)S(1)} %get-tuple-element.26), channel_id=1, source_target_pairs={{0,4},{4,0},{8,12},{12,8},{16,20},{20,16},{24,28},{28,24},{1,5},{5... | collective-permute-start | bytes 393224 | tf_op jit(solution)/shard_map/ppermute | solution.py:151
  11.4 10.8 %collective-permute-start.1 = (f32[4,16,512]{2,1,0:T(8,128)S(1)}, f32[4,16,512]{2,1,0:T(8,128)S(1)}, u32[]{:S(2)}, u32[]{:S(2)}) collective-permute-start(f32[4,16,512]{2,1,0:T(8,128)S(1)} %get-tuple-element.25), channel_id=1, source_target_pairs={{0,8},{4,12},{8,0},{12,4},{16,24},{20,28},{24,16},{28,20},{1,9},{5... | collective-permute-start | bytes 393224 | tf_op jit(solution)/shard_map/ppermute | solution.py:151
  13.0 10.0 %collective-permute-start.2 = (f32[4,16,512]{2,1,0:T(8,128)S(1)}, f32[4,16,512]{2,1,0:T(8,128)S(1)}, u32[]{:S(2)}, u32[]{:S(2)}) collective-permute-start(f32[4,16,512]{2,1,0:T(8,128)S(1)} %get-tuple-element.24), channel_id=1, source_target_pairs={{0,12},{4,8},{8,4},{12,0},{16,28},{20,24},{24,20},{28,16},{1,13},{... | collective-permute-start | bytes 393224 | tf_op jit(solution)/shard_map/ppermute | solution.py:151
  13.0 10.0 %collective-permute-start.3 = (f32[4,16,512]{2,1,0:T(8,128)S(1)}, f32[4,16,512]{2,1,0:T(8,128)S(1)}, u32[]{:S(2)}, u32[]{:S(2)}) collective-permute-start(f32[4,16,512]{2,1,0:T(8,128)S(1)} %get-tuple-element.23), channel_id=1, source_target_pairs={{0,16},{4,20},{8,24},{12,28},{16,0},{20,4},{24,8},{28,12},{1,17},{... | collective-permute-start | bytes 393224 | tf_op jit(solution)/shard_map/ppermute | solution.py:151
  16.0 19.4 %collective-permute-start.4 = (f32[4,16,512]{2,1,0:T(8,128)S(1)}, f32[4,16,512]{2,1,0:T(8,128)S(1)}, u32[]{:S(2)}, u32[]{:S(2)}) collective-permute-start(f32[4,16,512]{2,1,0:T(8,128)S(1)} %get-tuple-element.22), channel_id=1, source_target_pairs={{0,20},{4,16},{8,28},{12,24},{16,4},{20,0},{24,12},{28,8},{1,21},{... | collective-permute-start | bytes 393224 | tf_op jit(solution)/shard_map/ppermute | solution.py:151
  18.2 17.2 %collective-permute-start.5 = (f32[4,16,512]{2,1,0:T(8,128)S(1)}, f32[4,16,512]{2,1,0:T(8,128)S(1)}, u32[]{:S(2)}, u32[]{:S(2)}) collective-permute-start(f32[4,16,512]{2,1,0:T(8,128)S(1)} %get-tuple-element.21), channel_id=1, source_target_pairs={{0,24},{4,28},{8,16},{12,20},{16,8},{20,12},{24,0},{28,4},{1,25},{... | collective-permute-start | bytes 393224 | tf_op jit(solution)/shard_map/ppermute | solution.py:151
  22.1 13.3 %collective-permute-start.6 = (f32[4,16,512]{2,1,0:T(8,128)S(1)}, f32[4,16,512]{2,1,0:T(8,128)S(1)}, u32[]{:S(2)}, u32[]{:S(2)}) collective-permute-start(f32[4,16,512]{2,1,0:T(8,128)S(1)} %get-tuple-element.20), channel_id=1, source_target_pairs={{0,28},{4,24},{8,20},{12,16},{16,12},{20,8},{24,4},{28,0},{1,29},{... | collective-permute-start | bytes 393224 | tf_op jit(solution)/shard_map/ppermute | solution.py:151
  36.6 8.2 %collective-permute-start.7 = (f32[2,128,128]{2,1,0:T(8,128)S(1)}, f32[2,128,128]{2,1,0:T(8,128)S(1)}, u32[]{:S(2)}, u32[]{:S(2)}) collective-permute-start(f32[2,128,128]{2,1,0:T(8,128)S(1)} %constant_dynamic-slice_fusion.1), channel_id=1, source_target_pairs={{0,1},{1,0},{2,3},{3,2},{4,5},{5,4},{6,7},{7,6},{8,9},{9,8},{10,11... | collective-permute-start | bytes 393224 | tf_op jit(solution)/shard_map/ppermute | solution.py:151
  36.6 35.9 %all-to-all-start = ((f32[32,16,512]{2,1,0:T(8,128)}), f32[32,16,512]{2,1,0:T(8,128)}, u32[]{:S(2)}, u32[]{:S(2)}) async-start(f32[32,16,512]{2,1,0:T(8,128)} %bitcast.3), calls=%async_computation | async-start | bytes 2097152 | tf_op jit(solution)/shard_map/all_to_all | solution.py:195
  44.8 12.9 %collective-permute-start.8 = (f32[2,128,128]{2,1,0:T(8,128)S(1)}, f32[2,128,128]{2,1,0:T(8,128)S(1)}, u32[]{:S(2)}, u32[]{:S(2)}) collective-permute-start(f32[2,128,128]{2,1,0:T(8,128)S(1)} %dynamic-slice_add_fusion.1), channel_id=1, source_target_pairs={{0,2},{1,3},{2,0},{3,1},{4,6},{5,7},{6,4},{7,5},{8,10},{9,11},{10,... | collective-permute-start | bytes 393224 | tf_op jit(solution)/shard_map/ppermute | solution.py:151
  59.4 1.4 %collective-permute-start.9 = (f32[2,128,128]{2,1,0:T(8,128)S(1)}, f32[2,128,128]{2,1,0:T(8,128)S(1)}, u32[]{:S(2)}, u32[]{:S(2)}) collective-permute-start(f32[2,128,128]{2,1,0:T(8,128)S(1)} %convolution_multiply_fusion.3), channel_id=1, source_target_pairs={{0,1},{1,0},{2,3},{3,2},{4,5},{5,4},{6,7},{7,6},{8,9},{9,8},{10,11... | collective-permute-start | bytes 393224 | tf_op jit(solution)/shard_map/ppermute | solution.py:151
  62.9 1.4 %collective-permute-start.10 = (f32[2,128,128]{2,1,0:T(8,128)S(1)}, f32[2,128,128]{2,1,0:T(8,128)S(1)}, u32[]{:S(2)}, u32[]{:S(2)}) collective-permute-start(f32[2,128,128]{2,1,0:T(8,128)S(1)} %constant_dynamic-slice_fusion), channel_id=1, source_target_pairs={{0,1},{1,0},{2,3},{3,2},{4,5},{5,4},{6,7},{7,6},{8,9},{9,8},{10,11... | collective-permute-start | bytes 393224 | tf_op jit(solution)/shard_map/ppermute | solution.py:151
  64.3 7.3 %collective-permute-start.11 = (f32[2,128,128]{2,1,0:T(8,128)S(1)}, f32[2,128,128]{2,1,0:T(8,128)S(1)}, u32[]{:S(2)}, u32[]{:S(2)}) collective-permute-start(f32[2,128,128]{2,1,0:T(8,128)S(1)} %dynamic-slice_add_fusion), channel_id=1, source_target_pairs={{0,2},{1,3},{2,0},{3,1},{4,6},{5,7},{6,4},{7,5},{8,10},{9,11},{10,... | collective-permute-start | bytes 393224 | tf_op jit(solution)/shard_map/ppermute | solution.py:151
  80.7 31.3 %all-to-all-start.1 = ((f32[32,16,512]{2,1,0:T(8,128)}), f32[32,16,512]{2,1,0:T(8,128)}, u32[]{:S(2)}, u32[]{:S(2)}) async-start(f32[32,16,512]{2,1,0:T(8,128)} %shard_map.50), calls=%async_computation.1 | async-start | bytes 2097152 | tf_op jit(solution)/shard_map/all_to_all | solution.py:200
  85.2 1.7 %copy-start.3 = (f32[64,16,512]{2,1,0:T(8,128)S(1)}, f32[64,16,512]{2,1,0:T(8,128)}, u32[]{:S(2)}) copy-start(f32[64,16,512]{2,1,0:T(8,128)} %param.7) | copy-start | bytes 6291460
  86.9 1.4 %collective-permute-start.12 = (f32[2,128,128]{2,1,0:T(8,128)S(1)}, f32[2,128,128]{2,1,0:T(8,128)S(1)}, u32[]{:S(2)}, u32[]{:S(2)}) collective-permute-start(f32[2,128,128]{2,1,0:T(8,128)S(1)} %fusion.46), channel_id=1, source_target_pairs={{0,1},{1,0},{2,3},{3,2},{4,5},{5,4},{6,7},{7,6},{8,9},{9,8},{10,11... | collective-permute-start | bytes 393224 | tf_op jit(solution)/shard_map/ppermute | solution.py:151
  89.3 1.0 copy-start.2
  90.4 24.2 %collective-permute-start.13 = (f32[4,16,512]{2,1,0:T(8,128)S(1)}, f32[4,16,512]{2,1,0:T(8,128)}, u32[]{:S(2)}, u32[]{:S(2)}) collective-permute-start(f32[4,16,512]{2,1,0:T(8,128)S(1)} %get-tuple-element.33), channel_id=1, source_target_pairs={{0,4},{4,0},{8,12},{12,8},{16,20},{20,16},{24,28},{28,24},{1,5},{5... | collective-permute-start | bytes 393224 | tf_op jit(solution)/shard_map/ppermute | solution.py:151
  92.0 30.1 %collective-permute-start.14 = (f32[4,16,512]{2,1,0:T(8,128)S(1)}, f32[4,16,512]{2,1,0:T(8,128)S(1)}, u32[]{:S(2)}, u32[]{:S(2)}) collective-permute-start(f32[4,16,512]{2,1,0:T(8,128)S(1)} %get-tuple-element.32), channel_id=1, source_target_pairs={{0,8},{4,12},{8,0},{12,4},{16,24},{20,28},{24,16},{28,20},{1,9},{5... | collective-permute-start | bytes 393224 | tf_op jit(solution)/shard_map/ppermute | solution.py:151
  93.4 28.7 %collective-permute-start.15 = (f32[4,16,512]{2,1,0:T(8,128)S(1)}, f32[4,16,512]{2,1,0:T(8,128)S(1)}, u32[]{:S(2)}, u32[]{:S(2)}) collective-permute-start(f32[4,16,512]{2,1,0:T(8,128)S(1)} %get-tuple-element.31), channel_id=1, source_target_pairs={{0,12},{4,8},{8,4},{12,0},{16,28},{20,24},{24,20},{28,16},{1,13},{... | collective-permute-start | bytes 393224 | tf_op jit(solution)/shard_map/ppermute | solution.py:151
  93.9 28.3 %collective-permute-start.16 = (f32[4,16,512]{2,1,0:T(8,128)S(1)}, f32[4,16,512]{2,1,0:T(8,128)S(1)}, u32[]{:S(2)}, u32[]{:S(2)}) collective-permute-start(f32[4,16,512]{2,1,0:T(8,128)S(1)} %get-tuple-element.30), channel_id=1, source_target_pairs={{0,16},{4,20},{8,24},{12,28},{16,0},{20,4},{24,8},{28,12},{1,17},{... | collective-permute-start | bytes 393224 | tf_op jit(solution)/shard_map/ppermute | solution.py:151
  96.3 31.7 %collective-permute-start.17 = (f32[4,16,512]{2,1,0:T(8,128)S(1)}, f32[4,16,512]{2,1,0:T(8,128)S(1)}, u32[]{:S(2)}, u32[]{:S(2)}) collective-permute-start(f32[4,16,512]{2,1,0:T(8,128)S(1)} %get-tuple-element.29), channel_id=1, source_target_pairs={{0,20},{4,16},{8,28},{12,24},{16,4},{20,0},{24,12},{28,8},{1,21},{... | collective-permute-start | bytes 393224 | tf_op jit(solution)/shard_map/ppermute | solution.py:151
  114.6 13.5 %collective-permute-start.18 = (f32[4,16,512]{2,1,0:T(8,128)S(1)}, f32[4,16,512]{2,1,0:T(8,128)S(1)}, u32[]{:S(2)}, u32[]{:S(2)}) collective-permute-start(f32[4,16,512]{2,1,0:T(8,128)S(1)} %get-tuple-element.28), channel_id=1, source_target_pairs={{0,24},{4,28},{8,16},{12,20},{16,8},{20,12},{24,0},{28,4},{1,25},{... | collective-permute-start | bytes 393224 | tf_op jit(solution)/shard_map/ppermute | solution.py:151
  122.0 7.8 %collective-permute-start.19 = (f32[4,16,512]{2,1,0:T(8,128)S(1)}, f32[4,16,512]{2,1,0:T(8,128)S(1)}, u32[]{:S(2)}, u32[]{:S(2)}) collective-permute-start(f32[4,16,512]{2,1,0:T(8,128)S(1)} %get-tuple-element.27), channel_id=1, source_target_pairs={{0,28},{4,24},{8,20},{12,16},{16,12},{20,8},{24,4},{28,0},{1,29},{... | collective-permute-start | bytes 393224 | tf_op jit(solution)/shard_map/ppermute | solution.py:151
  129.9 1.3 %copy-start = (f32[8,8,16,512]{3,2,1,0:T(8,128)}, f32[8,8,16,512]{3,2,1,0:T(8,128)S(1)}, u32[]{:S(2)}) copy-start(f32[8,8,16,512]{3,2,1,0:T(8,128)S(1)} %fusion.18) | copy-start | bytes 6291460

commit v5 on v4

--- a/solution.py
+++ b/solution.py
@@ -157,7 +157,20 @@
     own = lax.dynamic_slice_in_dim(g, bit * half, half, 0)
     send = lax.dynamic_slice_in_dim(g, (1 - bit) * half, half, 0)
     own = own + swap(send, "model", model, 1)
-    return own + swap(own, "model", model, 2)
+    if half % 2:
+        return own + swap(own, "model", model, 2)
+    a, b = own[: half // 2], own[half // 2 :]
+    side = own.shape[1]
+    i = lax.broadcasted_iota(jnp.int32, (side, side), 0)
+    j = lax.broadcasted_iota(jnp.int32, (side, side), 1)
+    diagonal = jnp.einsum("mii->mi", b)[:, None, :]
+    pair = jnp.concatenate([jnp.where(i <= j, a, b), jnp.broadcast_to(diagonal, (half // 2, 8, side))], axis=1)
+    pair = swap(pair, "model", model, 2)
+    pair, diagonal = pair[:, :side], pair[:, side]
+    turned = pair.transpose(0, 2, 1)
+    a = a + jnp.where(i <= j, pair, turned)
+    b = b + jnp.where(i == j, diagonal[:, None, :], jnp.where(i > j, pair, turned))
+    return jnp.concatenate([a, b])
 
 
 def joined(own, model):
@@ -175,7 +188,7 @@
     x = mm(joined(q, model), x)
     g = summed(gram_of(x), model)
     q = joined(stacked_chain(g, ITERS - EARLY, eye), model)
-    return mm(q, x)
+    return jnp.einsum("mij,mjk->mik", q, x, precision=lax.Precision.HIGH)
 
 
 def direct(blocks, shards):

time: 134 us -> 139 us (1.037)
  waiting for transfers between devices: 55.4 us -> 60.9 us
    all_to_all x1, waiting for transfers between devices: 0.01 us -> 13.4 us  [mixed(): lax.all_to_all(first.reshape(shards * model, rows, cols), AXES, split_axi...]
    ppermute x20, waiting for transfers between devices: 41.2 us -> 33 us  [swap(): return lax.ppermute(x, axis, [(i, i ^ bits) for i in range(size)])]
    dot_general x16 -> x15, matrix products: 5.88 us -> 4.88 us  [mm(): return jnp.einsum('mij,mjk->mik', a, b, precision=HI)]
  transfers between devices with their start and end apart: 22 -> 22, of which waited for: 10 -> 11; matrix products, arithmetic and copies ran while one was open for 9% -> 8% of each run, Pallas kernels for 0% -> 0%
where the time goes in v5:
time: 139 us; the launch traced here: 137 us
  waiting for transfers between devices  60.9 us (44%)
  starting transfers between devices  43.2 us (31%)
  other arithmetic  10.6 us (8%)
  Pallas kernels  8.17 us (6%)
  matrix products  7.67 us (6%)
  local copies, waits for them, and re-layouts  4.91 us (4%)
    ppermute x20, waiting for transfers between devices, swap(): return lax.ppermute(x, axis, [(i, i ^ bits) for i in range(size)])  33 us
    ppermute x20, starting transfers between devices, swap(): return lax.ppermute(x, axis, [(i, i ^ bits) for i in range(size)])  31.2 us
    all_to_all x1, waiting for transfers between devices, mixed(): first = lax.all_to_all(first, AXES, split_axis=0, concat_axis=0, tiled=True)  14.6 us
    all_to_all x1, waiting for transfers between devices, mixed(): lax.all_to_all(first.reshape(shards * model, rows, cols), AXES, split_axi...  13.4 us
    pallas_call x1, Pallas kernels, whole(): pl.pallas_call(functools.partial(whole_kernel, shards, model, rows, cols)...  8.17 us
    all_to_all x1, starting transfers between devices, mixed(): lax.all_to_all(first.reshape(shards * model, rows, cols), AXES, split_axi...  8.11 us
    dot_general x15, matrix products, mm(): return jnp.einsum('mij,mjk->mik', a, b, precision=HI)  4.88 us
    all_to_all x1, starting transfers between devices, mixed(): first = lax.all_to_all(first, AXES, split_axis=0, concat_axis=0, tiled=True)  3.96 us
  transfers between devices with their start and end apart: 22, of which 11 were waited for; matrix products, arithmetic and copies ran while one was open for 8% of the time, Pallas kernels for 0%

profile of v5, /device:TPU:0, one launch (start us, length us, event | category | flops | bytes accessed | tf_op | source)
XLA Modules:
  0.0 136.7 jit_solution(16257292150830700881)
XLA Ops:
  0.7 3.0 %slice_add_fusion = f32[8,4,16,512]{3,2,1,0:T(8,128)} fusion(f32[8,8,16,512]{3,2,1,0:T(8,128)} %bitcast.159, f32[8,8,16,512]{3,2,1,0:T(8,128)} %bitcast.160), kind=kLoop, calls=%fused_computation.12 | loop fusion | flops 524288 | bytes 3145728 | tf_op jit(solution)/shard_map/add | solution.py:204
  3.6 3.4 %multiply_add_fusion = f32[64,16,512]{2,1,0:T(8,128)} fusion(f32[64,16,512]{2,1,0:T(8,128)S(1)} %copy-done.1, f32[64,16,512]{2,1,0:T(8,128)} %param.6), kind=kLoop, calls=%fused_computation | loop fusion | flops 1048576 | bytes 6291456 | tf_op jit(solution)/shard_map/add | solution.py:206
  7.0 1.3 dynamic-slice_bitcast_fusion
  8.3 3.0 %collective-permute-start = (f32[4,16,512]{2,1,0:T(8,128)S(1)}, f32[4,16,512]{2,1,0:T(8,128)S(1)}, u32[]{:S(2)}, u32[]{:S(2)}) collective-permute-start(f32[4,16,512]{2,1,0:T(8,128)S(1)} %get-tuple-element.24), channel_id=1, source_target_pairs={{0,4},{4,0},{8,12},{12,8},{16,20},{20,16},{24,28},{28,24},{1,5},{5... | collective-permute-start | bytes 393224 | tf_op jit(solution)/shard_map/ppermute | solution.py:151
  11.4 1.6 %collective-permute-start.1 = (f32[4,16,512]{2,1,0:T(8,128)S(1)}, f32[4,16,512]{2,1,0:T(8,128)S(1)}, u32[]{:S(2)}, u32[]{:S(2)}) collective-permute-start(f32[4,16,512]{2,1,0:T(8,128)S(1)} %get-tuple-element.23), channel_id=1, source_target_pairs={{0,8},{4,12},{8,0},{12,4},{16,24},{20,28},{24,16},{28,20},{1,9},{5... | collective-permute-start | bytes 393224 | tf_op jit(solution)/shard_map/ppermute | solution.py:151
  13.0 3.0 %collective-permute-start.3 = (f32[4,16,512]{2,1,0:T(8,128)S(1)}, f32[4,16,512]{2,1,0:T(8,128)S(1)}, u32[]{:S(2)}, u32[]{:S(2)}) collective-permute-start(f32[4,16,512]{2,1,0:T(8,128)S(1)} %get-tuple-element.21), channel_id=1, source_target_pairs={{0,16},{4,20},{8,24},{12,28},{16,0},{20,4},{24,8},{28,12},{1,17},{... | collective-permute-start | bytes 393224 | tf_op jit(solution)/shard_map/ppermute | solution.py:151
  16.0 1.3 collective-permute-start.4
  17.3 0.9 bitcast_dynamic-update-slice_fusion
  18.2 3.7 %collective-permute-start.5 = (f32[4,16,512]{2,1,0:T(8,128)S(1)}, f32[4,16,512]{2,1,0:T(8,128)S(1)}, u32[]{:S(2)}, u32[]{:S(2)}) collective-permute-start(f32[4,16,512]{2,1,0:T(8,128)S(1)} %get-tuple-element.19), channel_id=1, source_target_pairs={{0,24},{4,28},{8,16},{12,20},{16,8},{20,12},{24,0},{28,4},{1,25},{... | collective-permute-start | bytes 393224 | tf_op jit(solution)/shard_map/ppermute | solution.py:151
  21.9 0.3 collective-permute-done.1
  22.1 0.8 collective-permute-start.6
  23.0 12.4 %collective-permute-done.4 = f32[4,16,512]{2,1,0:T(8,128)S(1)} collective-permute-done((f32[4,16,512]{2,1,0:T(8,128)S(1)}, f32[4,16,512]{2,1,0:T(8,128)S(1)}, u32[]{:S(2)}, u32[]{:S(2)}) %collective-permute-start.4) | collective-permute-done | bytes 131104 | tf_op jit(solution)/shard_map/ppermute | solution.py:151
  35.4 1.1 fusion.51
  36.6 0.1 collective-permute-start.7
  36.7 1.3 collective-permute-done.7
  38.1 1.6 %collective-permute-start.8 = (f32[1,136,128]{2,1,0:T(8,128)S(1)}, f32[1,136,128]{2,1,0:T(8,128)S(1)}, u32[]{:S(2)}, u32[]{:S(2)}) collective-permute-start(f32[1,136,128]{2,1,0:T(8,128)S(1)} %pad_maximum_fusion.6), channel_id=1, source_target_pairs={{0,2},{1,3},{2,0},{3,1},{4,6},{5,7},{6,4},{7,5},{8,10},{9,11},{10,... | collective-permute-start | bytes 208904 | tf_op jit(solution)/shard_map/ppermute | solution.py:151
  39.7 2.8 %collective-permute-done.8 = f32[1,136,128]{2,1,0:T(8,128)S(1)} collective-permute-done((f32[1,136,128]{2,1,0:T(8,128)S(1)}, f32[1,136,128]{2,1,0:T(8,128)S(1)}, u32[]{:S(2)}, u32[]{:S(2)}) %collective-permute-start.8) | collective-permute-done | bytes 69664 | tf_op jit(solution)/shard_map/ppermute | solution.py:151
  42.4 0.1 copy.6
  42.6 0.1 select_reduce_fusion
  42.7 0.3 fusion.4
  43.1 0.3 fusion.30
  43.4 0.3 fusion.52
  43.7 0.3 fusion.3
  43.9 0.3 convolution_multiply_fusion.3
  44.3 8.1 %all-to-all-start = ((f32[32,16,512]{2,1,0:T(8,128)}), f32[32,16,512]{2,1,0:T(8,128)}, u32[]{:S(2)}, u32[]{:S(2)}) async-start(f32[32,16,512]{2,1,0:T(8,128)} %bitcast.3), calls=%async_computation | async-start | bytes 2097152 | tf_op jit(solution)/shard_map/all_to_all | solution.py:208
  52.4 1.0 fusion.6
  53.4 1.1 fusion.53
  54.6 0.2 collective-permute-start.10
  54.8 1.2 collective-permute-done.10
  56.1 1.8 %collective-permute-start.11 = (f32[1,136,128]{2,1,0:T(8,128)S(1)}, f32[1,136,128]{2,1,0:T(8,128)S(1)}, u32[]{:S(2)}, u32[]{:S(2)}) collective-permute-start(f32[1,136,128]{2,1,0:T(8,128)S(1)} %pad_maximum_fusion.7), channel_id=1, source_target_pairs={{0,2},{1,3},{2,0},{3,1},{4,6},{5,7},{6,4},{7,5},{8,10},{9,11},{10,... | collective-permute-start | bytes 208904 | tf_op jit(solution)/shard_map/ppermute | solution.py:151
  57.8 6.4 %collective-permute-done.11 = f32[1,136,128]{2,1,0:T(8,128)S(1)} collective-permute-done((f32[1,136,128]{2,1,0:T(8,128)S(1)}, f32[1,136,128]{2,1,0:T(8,128)S(1)}, u32[]{:S(2)}, u32[]{:S(2)}) %collective-permute-start.11) | collective-permute-done | bytes 69664 | tf_op jit(solution)/shard_map/ppermute | solution.py:151
  64.3 0.1 copy.7
  64.4 0.3 fusion.2
  64.7 0.3 fusion.32
  64.9 0.3 fusion.54
  65.2 13.4 %all-to-all-done.x_ref = f32[32,16,512]{2,1,0:T(8,128)} async-done(((f32[32,16,512]{2,1,0:T(8,128)}), f32[32,16,512]{2,1,0:T(8,128)}, u32[]{:S(2)}, u32[]{:S(2)}) %all-to-all-start) | async-done | bytes 1048608 | tf_op jit(solution)/shard_map/all_to_all | solution.py:208
  78.6 8.2 %shard_map.50 = f32[32,16,512]{2,1,0:T(8,128)} custom-call(f32[32,16,512]{2,1,0:T(8,128)} %all-to-all-done.x_ref), custom_call_target="tpu_custom_call" | custom-call | flops 1610612736 | bytes 2097152 | tf_op jit(solution)/shard_map/pallas_call | solution.py:122
  86.8 4.0 %all-to-all-start.1 = ((f32[32,16,512]{2,1,0:T(8,128)}), f32[32,16,512]{2,1,0:T(8,128)}, u32[]{:S(2)}, u32[]{:S(2)}) async-start(f32[32,16,512]{2,1,0:T(8,128)} %shard_map.50), calls=%async_computation.1 | async-start | bytes 2097152 | tf_op jit(solution)/shard_map/all_to_all | solution.py:213
  90.7 0.3 fusion.1
  91.0 0.3 fusion.55
  91.3 0.3 fusion.57
  91.6 0.3 fusion.56
  91.8 0.3 fusion
  92.1 0.3 fusion.58
  92.4 0.1 collective-permute-start.12
  92.5 0.2 broadcast_multiply_fusion
  92.7 1.1 collective-permute-done.12
  93.8 0.6 fusion.12
  94.4 1.0 copy-done.2
  95.4 0.1 slice_bitcast_fusion
  95.5 1.6 %collective-permute-start.13 = (f32[4,16,512]{2,1,0:T(8,128)S(1)}, f32[4,16,512]{2,1,0:T(8,128)}, u32[]{:S(2)}, u32[]{:S(2)}) collective-permute-start(f32[4,16,512]{2,1,0:T(8,128)S(1)} %get-tuple-element.31), channel_id=1, source_target_pairs={{0,4},{4,0},{8,12},{12,8},{16,20},{20,16},{24,28},{28,24},{1,5},{5... | collective-permute-start | bytes 393224 | tf_op jit(solution)/shard_map/ppermute | solution.py:151
  97.1 1.5 %collective-permute-start.14 = (f32[4,16,512]{2,1,0:T(8,128)S(1)}, f32[4,16,512]{2,1,0:T(8,128)S(1)}, u32[]{:S(2)}, u32[]{:S(2)}) collective-permute-start(f32[4,16,512]{2,1,0:T(8,128)S(1)} %get-tuple-element.30), channel_id=1, source_target_pairs={{0,8},{4,12},{8,0},{12,4},{16,24},{20,28},{24,16},{28,20},{1,9},{5... | collective-permute-start | bytes 393224 | tf_op jit(solution)/shard_map/ppermute | solution.py:151
  98.5 0.5 collective-permute-start.15
  99.0 2.4 %collective-permute-start.16 = (f32[4,16,512]{2,1,0:T(8,128)S(1)}, f32[4,16,512]{2,1,0:T(8,128)S(1)}, u32[]{:S(2)}, u32[]{:S(2)}) collective-permute-start(f32[4,16,512]{2,1,0:T(8,128)S(1)} %get-tuple-element.28), channel_id=1, source_target_pairs={{0,16},{4,20},{8,24},{12,28},{16,0},{20,4},{24,8},{28,12},{1,17},{... | collective-permute-start | bytes 393224 | tf_op jit(solution)/shard_map/ppermute | solution.py:151
  101.5 1.5 %collective-permute-start.17 = (f32[4,16,512]{2,1,0:T(8,128)S(1)}, f32[4,16,512]{2,1,0:T(8,128)S(1)}, u32[]{:S(2)}, u32[]{:S(2)}) collective-permute-start(f32[4,16,512]{2,1,0:T(8,128)S(1)} %get-tuple-element.27), channel_id=1, source_target_pairs={{0,20},{4,16},{8,28},{12,24},{16,4},{20,0},{24,12},{28,8},{1,21},{... | collective-permute-start | bytes 393224 | tf_op jit(solution)/shard_map/ppermute | solution.py:151
  102.9 14.6 %all-to-all-done.1 = f32[32,16,512]{2,1,0:T(8,128)} async-done(((f32[32,16,512]{2,1,0:T(8,128)}), f32[32,16,512]{2,1,0:T(8,128)}, u32[]{:S(2)}, u32[]{:S(2)}) %all-to-all-start.1) | async-done | bytes 1048608 | tf_op jit(solution)/shard_map/all_to_all | solution.py:213
  117.5 1.3 broadcast_multiply_fusion.1
  118.8 0.3 fusion.5
  119.1 0.9 fusion.19
  120.1 6.5 %collective-permute-start.18 = (f32[4,16,512]{2,1,0:T(8,128)S(1)}, f32[4,16,512]{2,1,0:T(8,128)S(1)}, u32[]{:S(2)}, u32[]{:S(2)}) collective-permute-start(f32[4,16,512]{2,1,0:T(8,128)S(1)} %get-tuple-element.26), channel_id=1, source_target_pairs={{0,24},{4,28},{8,16},{12,20},{16,8},{20,12},{24,0},{28,4},{1,25},{... | collective-permute-start | bytes 393224 | tf_op jit(solution)/shard_map/ppermute | solution.py:151
  126.6 0.9 fusion.26
  127.7 5.8 %collective-permute-done.17 = f32[4,16,512]{2,1,0:T(8,128)S(1)} collective-permute-done((f32[4,16,512]{2,1,0:T(8,128)S(1)}, f32[4,16,512]{2,1,0:T(8,128)S(1)}, u32[]{:S(2)}, u32[]{:S(2)}) %collective-permute-start.17) | collective-permute-done | bytes 131104 | tf_op jit(solution)/shard_map/ppermute | solution.py:151
  133.6 1.7 %collective-permute-done.19 = f32[4,16,512]{2,1,0:T(8,128)S(1)} collective-permute-done((f32[4,16,512]{2,1,0:T(8,128)S(1)}, f32[4,16,512]{2,1,0:T(8,128)S(1)}, u32[]{:S(2)}, u32[]{:S(2)}) %collective-permute-start.19) | collective-permute-done | bytes 131104 | tf_op jit(solution)/shard_map/ppermute | solution.py:151
  135.4 1.3 copy-done
  (53 shorter events, 0.7 us)
Async XLA Ops:
  0.6 3.0 %copy-start.1 = (f32[64,16,512]{2,1,0:T(8,128)S(1)}, f32[64,16,512]{2,1,0:T(8,128)}, u32[]{:S(2)}) copy-start(f32[64,16,512]{2,1,0:T(8,128)} %param.5) | copy-start | bytes 6291460
  8.3 9.8 %collective-permute-start = (f32[4,16,512]{2,1,0:T(8,128)S(1)}, f32[4,16,512]{2,1,0:T(8,128)S(1)}, u32[]{:S(2)}, u32[]{:S(2)}) collective-permute-start(f32[4,16,512]{2,1,0:T(8,128)S(1)} %get-tuple-element.24), channel_id=1, source_target_pairs={{0,4},{4,0},{8,12},{12,8},{16,20},{20,16},{24,28},{28,24},{1,5},{5... | collective-permute-start | bytes 393224 | tf_op jit(solution)/shard_map/ppermute | solution.py:151
  11.4 10.8 %collective-permute-start.1 = (f32[4,16,512]{2,1,0:T(8,128)S(1)}, f32[4,16,512]{2,1,0:T(8,128)S(1)}, u32[]{:S(2)}, u32[]{:S(2)}) collective-permute-start(f32[4,16,512]{2,1,0:T(8,128)S(1)} %get-tuple-element.23), channel_id=1, source_target_pairs={{0,8},{4,12},{8,0},{12,4},{16,24},{20,28},{24,16},{28,20},{1,9},{5... | collective-permute-start | bytes 393224 | tf_op jit(solution)/shard_map/ppermute | solution.py:151
  13.0 10.0 %collective-permute-start.2 = (f32[4,16,512]{2,1,0:T(8,128)S(1)}, f32[4,16,512]{2,1,0:T(8,128)S(1)}, u32[]{:S(2)}, u32[]{:S(2)}) collective-permute-start(f32[4,16,512]{2,1,0:T(8,128)S(1)} %get-tuple-element.22), channel_id=1, source_target_pairs={{0,12},{4,8},{8,4},{12,0},{16,28},{20,24},{24,20},{28,16},{1,13},{... | collective-permute-start | bytes 393224 | tf_op jit(solution)/shard_map/ppermute | solution.py:151
  13.0 10.0 %collective-permute-start.3 = (f32[4,16,512]{2,1,0:T(8,128)S(1)}, f32[4,16,512]{2,1,0:T(8,128)S(1)}, u32[]{:S(2)}, u32[]{:S(2)}) collective-permute-start(f32[4,16,512]{2,1,0:T(8,128)S(1)} %get-tuple-element.21), channel_id=1, source_target_pairs={{0,16},{4,20},{8,24},{12,28},{16,0},{20,4},{24,8},{28,12},{1,17},{... | collective-permute-start | bytes 393224 | tf_op jit(solution)/shard_map/ppermute | solution.py:151
  16.0 19.4 %collective-permute-start.4 = (f32[4,16,512]{2,1,0:T(8,128)S(1)}, f32[4,16,512]{2,1,0:T(8,128)S(1)}, u32[]{:S(2)}, u32[]{:S(2)}) collective-permute-start(f32[4,16,512]{2,1,0:T(8,128)S(1)} %get-tuple-element.20), channel_id=1, source_target_pairs={{0,20},{4,16},{8,28},{12,24},{16,4},{20,0},{24,12},{28,8},{1,21},{... | collective-permute-start | bytes 393224 | tf_op jit(solution)/shard_map/ppermute | solution.py:151
  18.2 17.2 %collective-permute-start.5 = (f32[4,16,512]{2,1,0:T(8,128)S(1)}, f32[4,16,512]{2,1,0:T(8,128)S(1)}, u32[]{:S(2)}, u32[]{:S(2)}) collective-permute-start(f32[4,16,512]{2,1,0:T(8,128)S(1)} %get-tuple-element.19), channel_id=1, source_target_pairs={{0,24},{4,28},{8,16},{12,20},{16,8},{20,12},{24,0},{28,4},{1,25},{... | collective-permute-start | bytes 393224 | tf_op jit(solution)/shard_map/ppermute | solution.py:151
  22.1 13.3 %collective-permute-start.6 = (f32[4,16,512]{2,1,0:T(8,128)S(1)}, f32[4,16,512]{2,1,0:T(8,128)S(1)}, u32[]{:S(2)}, u32[]{:S(2)}) collective-permute-start(f32[4,16,512]{2,1,0:T(8,128)S(1)} %get-tuple-element.18), channel_id=1, source_target_pairs={{0,28},{4,24},{8,20},{12,16},{16,12},{20,8},{24,4},{28,0},{1,29},{... | collective-permute-start | bytes 393224 | tf_op jit(solution)/shard_map/ppermute | solution.py:151
  36.6 1.4 %collective-permute-start.7 = (f32[2,128,128]{2,1,0:T(8,128)S(1)}, f32[2,128,128]{2,1,0:T(8,128)S(1)}, u32[]{:S(2)}, u32[]{:S(2)}) collective-permute-start(f32[2,128,128]{2,1,0:T(8,128)S(1)} %constant_dynamic-slice_fusion.1), channel_id=1, source_target_pairs={{0,1},{1,0},{2,3},{3,2},{4,5},{5,4},{6,7},{7,6},{8,9},{9,8},{10,11... | collective-permute-start | bytes 393224 | tf_op jit(solution)/shard_map/ppermute | solution.py:151
  38.1 4.4 %collective-permute-start.8 = (f32[1,136,128]{2,1,0:T(8,128)S(1)}, f32[1,136,128]{2,1,0:T(8,128)S(1)}, u32[]{:S(2)}, u32[]{:S(2)}) collective-permute-start(f32[1,136,128]{2,1,0:T(8,128)S(1)} %pad_maximum_fusion.6), channel_id=1, source_target_pairs={{0,2},{1,3},{2,0},{3,1},{4,6},{5,7},{6,4},{7,5},{8,10},{9,11},{10,... | collective-permute-start | bytes 208904 | tf_op jit(solution)/shard_map/ppermute | solution.py:151
  44.2 8.2 %collective-permute-start.9 = (f32[2,128,128]{2,1,0:T(8,128)S(1)}, f32[2,128,128]{2,1,0:T(8,128)S(1)}, u32[]{:S(2)}, u32[]{:S(2)}) collective-permute-start(f32[2,128,128]{2,1,0:T(8,128)S(1)} %convolution_multiply_fusion.3), channel_id=1, source_target_pairs={{0,1},{1,0},{2,3},{3,2},{4,5},{5,4},{6,7},{7,6},{8,9},{9,8},{10,11... | collective-permute-start | bytes 393224 | tf_op jit(solution)/shard_map/ppermute | solution.py:151
  44.3 34.3 %all-to-all-start = ((f32[32,16,512]{2,1,0:T(8,128)}), f32[32,16,512]{2,1,0:T(8,128)}, u32[]{:S(2)}, u32[]{:S(2)}) async-start(f32[32,16,512]{2,1,0:T(8,128)} %bitcast.3), calls=%async_computation | async-start | bytes 2097152 | tf_op jit(solution)/shard_map/all_to_all | solution.py:208
  54.6 1.4 %collective-permute-start.10 = (f32[2,128,128]{2,1,0:T(8,128)S(1)}, f32[2,128,128]{2,1,0:T(8,128)S(1)}, u32[]{:S(2)}, u32[]{:S(2)}) collective-permute-start(f32[2,128,128]{2,1,0:T(8,128)S(1)} %constant_dynamic-slice_fusion), channel_id=1, source_target_pairs={{0,1},{1,0},{2,3},{3,2},{4,5},{5,4},{6,7},{7,6},{8,9},{9,8},{10,11... | collective-permute-start | bytes 393224 | tf_op jit(solution)/shard_map/ppermute | solution.py:151
  56.1 8.2 %collective-permute-start.11 = (f32[1,136,128]{2,1,0:T(8,128)S(1)}, f32[1,136,128]{2,1,0:T(8,128)S(1)}, u32[]{:S(2)}, u32[]{:S(2)}) collective-permute-start(f32[1,136,128]{2,1,0:T(8,128)S(1)} %pad_maximum_fusion.7), channel_id=1, source_target_pairs={{0,2},{1,3},{2,0},{3,1},{4,6},{5,7},{6,4},{7,5},{8,10},{9,11},{10,... | collective-permute-start | bytes 208904 | tf_op jit(solution)/shard_map/ppermute | solution.py:151
  86.8 30.7 %all-to-all-start.1 = ((f32[32,16,512]{2,1,0:T(8,128)}), f32[32,16,512]{2,1,0:T(8,128)}, u32[]{:S(2)}, u32[]{:S(2)}) async-start(f32[32,16,512]{2,1,0:T(8,128)} %shard_map.50), calls=%async_computation.1 | async-start | bytes 2097152 | tf_op jit(solution)/shard_map/all_to_all | solution.py:213
  90.7 1.7 %copy-start.3 = (f32[64,16,512]{2,1,0:T(8,128)S(1)}, f32[64,16,512]{2,1,0:T(8,128)}, u32[]{:S(2)}) copy-start(f32[64,16,512]{2,1,0:T(8,128)} %param.7) | copy-start | bytes 6291460
  92.4 1.4 %collective-permute-start.12 = (f32[2,128,128]{2,1,0:T(8,128)S(1)}, f32[2,128,128]{2,1,0:T(8,128)S(1)}, u32[]{:S(2)}, u32[]{:S(2)}) collective-permute-start(f32[2,128,128]{2,1,0:T(8,128)S(1)} %fusion.58), channel_id=1, source_target_pairs={{0,1},{1,0},{2,3},{3,2},{4,5},{5,4},{6,7},{7,6},{8,9},{9,8},{10,11... | collective-permute-start | bytes 393224 | tf_op jit(solution)/shard_map/ppermute | solution.py:151
  94.4 1.0 copy-start.2
  95.5 24.6 %collective-permute-start.13 = (f32[4,16,512]{2,1,0:T(8,128)S(1)}, f32[4,16,512]{2,1,0:T(8,128)}, u32[]{:S(2)}, u32[]{:S(2)}) collective-permute-start(f32[4,16,512]{2,1,0:T(8,128)S(1)} %get-tuple-element.31), channel_id=1, source_target_pairs={{0,4},{4,0},{8,12},{12,8},{16,20},{20,16},{24,28},{28,24},{1,5},{5... | collective-permute-start | bytes 393224 | tf_op jit(solution)/shard_map/ppermute | solution.py:151
  97.1 30.5 %collective-permute-start.14 = (f32[4,16,512]{2,1,0:T(8,128)S(1)}, f32[4,16,512]{2,1,0:T(8,128)S(1)}, u32[]{:S(2)}, u32[]{:S(2)}) collective-permute-start(f32[4,16,512]{2,1,0:T(8,128)S(1)} %get-tuple-element.30), channel_id=1, source_target_pairs={{0,8},{4,12},{8,0},{12,4},{16,24},{20,28},{24,16},{28,20},{1,9},{5... | collective-permute-start | bytes 393224 | tf_op jit(solution)/shard_map/ppermute | solution.py:151
  98.5 29.1 %collective-permute-start.15 = (f32[4,16,512]{2,1,0:T(8,128)S(1)}, f32[4,16,512]{2,1,0:T(8,128)S(1)}, u32[]{:S(2)}, u32[]{:S(2)}) collective-permute-start(f32[4,16,512]{2,1,0:T(8,128)S(1)} %get-tuple-element.29), channel_id=1, source_target_pairs={{0,12},{4,8},{8,4},{12,0},{16,28},{20,24},{24,20},{28,16},{1,13},{... | collective-permute-start | bytes 393224 | tf_op jit(solution)/shard_map/ppermute | solution.py:151
  99.0 28.7 %collective-permute-start.16 = (f32[4,16,512]{2,1,0:T(8,128)S(1)}, f32[4,16,512]{2,1,0:T(8,128)S(1)}, u32[]{:S(2)}, u32[]{:S(2)}) collective-permute-start(f32[4,16,512]{2,1,0:T(8,128)S(1)} %get-tuple-element.28), channel_id=1, source_target_pairs={{0,16},{4,20},{8,24},{12,28},{16,0},{20,4},{24,8},{28,12},{1,17},{... | collective-permute-start | bytes 393224 | tf_op jit(solution)/shard_map/ppermute | solution.py:151
  101.5 32.1 %collective-permute-start.17 = (f32[4,16,512]{2,1,0:T(8,128)S(1)}, f32[4,16,512]{2,1,0:T(8,128)S(1)}, u32[]{:S(2)}, u32[]{:S(2)}) collective-permute-start(f32[4,16,512]{2,1,0:T(8,128)S(1)} %get-tuple-element.27), channel_id=1, source_target_pairs={{0,20},{4,16},{8,28},{12,24},{16,4},{20,0},{24,12},{28,8},{1,21},{... | collective-permute-start | bytes 393224 | tf_op jit(solution)/shard_map/ppermute | solution.py:151
  120.1 13.5 %collective-permute-start.18 = (f32[4,16,512]{2,1,0:T(8,128)S(1)}, f32[4,16,512]{2,1,0:T(8,128)S(1)}, u32[]{:S(2)}, u32[]{:S(2)}) collective-permute-start(f32[4,16,512]{2,1,0:T(8,128)S(1)} %get-tuple-element.26), channel_id=1, source_target_pairs={{0,24},{4,28},{8,16},{12,20},{16,8},{20,12},{24,0},{28,4},{1,25},{... | collective-permute-start | bytes 393224 | tf_op jit(solution)/shard_map/ppermute | solution.py:151
  127.5 7.8 %collective-permute-start.19 = (f32[4,16,512]{2,1,0:T(8,128)S(1)}, f32[4,16,512]{2,1,0:T(8,128)S(1)}, u32[]{:S(2)}, u32[]{:S(2)}) collective-permute-start(f32[4,16,512]{2,1,0:T(8,128)S(1)} %get-tuple-element.25), channel_id=1, source_target_pairs={{0,28},{4,24},{8,20},{12,16},{16,12},{20,8},{24,4},{28,0},{1,29},{... | collective-permute-start | bytes 393224 | tf_op jit(solution)/shard_map/ppermute | solution.py:151
  135.4 1.3 copy-start
